TPU v7x, 32 devices: a whole 2x2x4 slice. The times are simulated.
32 devices in a mesh: grp: 4 (over y, core), blk: 8 (over z, x).
Axes of the slice: x: 2, y: 2, z: 4, core: 2. Of those that a mesh axis runs over, the one named last changes fastest.
Arguments:
- primal: float32 [262144], P(('blk', 'grp')), may hold values from -3 to 3
- dual: float32 [131072], P(('blk', 'grp')), may hold values from -3 to 3
- objective: float32 [262144], P(('blk', 'grp')), may hold values from -6 to 6
- lower: float32 [262144], P(('blk', 'grp')), may hold values from -2 to -0.5
- upper: float32 [262144], P(('blk', 'grp')), may hold values from 0.5 to 2
- bound_kind: int32 [262144], P(('blk', 'grp')), may hold values from 0 to 3
- rhs: float32 [131072], P(('blk', 'grp')), may hold values from -6 to 6
- row_kind: int32 [131072], P(('blk', 'grp')), may hold values 0 or 1
- q_tiles: float32 [4, 32, 512, 512], P('grp', 'blk'), may hold values from -0.25 to 0.25
- q_index: int32 [4, 2, 32], P('grp', None, 'blk'), may hold values from 0 to 127
- k_tiles: float32 [4, 48, 512, 512], P('grp', 'blk'), may hold values from -0.25 to 0.25
- k_rows: int32 [4, 48], P('grp', 'blk'), may hold values from 0 to 31
- k_cols: int32 [4, 48], P('grp', 'blk'), may hold values from 0 to 127
Outputs:
- final_primal: float32 [262144], P(('blk', 'grp'))
- final_dual: float32 [131072], P(('blk', 'grp'))
- primal_weight: float32 [], replicated
Inputs may be any that keep to these rules, and one draw needn't show every extreme that they name: `q_index`: row and column tile indices of Hessian tiles, within the column group. `k_rows`: row tile within the tile's dual block. `bound_kind`: 0 free, 1 lower bound only, 2 both bounds, 3 upper bound only.
All inputs are finite; a program needn't handle non-finite values. No bound on the sum of `row_kind` on one device may be relied on, other than what follows from the above.
Results may differ from a plain program's by a relative error of at most 0.00017.
Values sent between devices are 32-bit elements; how exact they have to be, the bound alone decides.
A program may use at most 64 MiB of HBM per device.

v0:
```python
import functools

import jax
import jax.numpy as jnp
from jax import lax
from jax.experimental import pallas as pl
from jax.experimental.pallas import tpu as pltpu
from jax.sharding import PartitionSpec as P

ITERS = 2
EPSILON = 1e-06
STEP_SCALE = 0.5
LANES = 128
CHUNK = 512
MESH = pl.DeviceIdType.MESH
F32 = jnp.float32
BF16 = jnp.bfloat16


def split(values):
    high = values.astype(BF16)
    return high, (values - high.astype(F32)).astype(BF16)


def exchange(axis, count, me, source, target, send, recv):
    def copy(k, slot):
        peer = lax.rem(me + k, count)
        return pltpu.make_async_remote_copy(
            src_ref=source,
            dst_ref=target(me if slot else peer),
            send_sem=send.at[k],
            recv_sem=recv.at[me if slot else peer],
            device_id={axis: peer},
            device_id_type=MESH,
        )

    def start(k, carry):
        copy(k, True).start()
        return carry

    def arrive(k, carry):
        copy(k, False).wait_recv()
        return carry

    def leave(k, carry):
        copy(k, True).wait_send()
        return carry

    lax.fori_loop(1, count, start, 0)
    return (
        lambda: lax.fori_loop(1, count, arrive, 0),
        lambda: lax.fori_loop(1, count, leave, 0),
    )


def segment(ids, start, width, rows, quarters):
    place = lax.broadcasted_iota(jnp.int32, (rows, LANES), 0) * LANES
    place = place + lax.broadcasted_iota(jnp.int32, (rows, LANES), 1) - start
    result = jnp.full((rows, LANES), -1, jnp.int32)
    for p, tile_id in enumerate(ids):
        for q in range(quarters):
            result = jnp.where(place == p * quarters + q, tile_id * quarters + q, result)
    return jnp.where((place >= 0) & (place < width), result, 0)


def kernel(
    n_blk,
    n_grp,
    primal,
    dual,
    objective,
    lower,
    upper,
    bound_kind,
    rhs,
    row_kind,
    q_index,
    k_rows,
    k_cols,
    q_tiles,
    k_tiles,
    x_out,
    y_out,
    w_out,
    raw,
    whi,
    wlo,
    xs,
    ys,
    data,
    rows_data,
    ids_x,
    ids_y,
    sel_h,
    sel_t,
    sel_y,
    vals_h,
    vals_t,
    vals_y,
    sums_x,
    sums_y,
    cons_now,
    tile_sem,
    blk_send,
    blk_recv,
    grp_send,
    grp_recv,
):
    blk, grp = lax.axis_index("blk"), lax.axis_index("grp")
    nq, nk = q_tiles.shape[0], k_tiles.shape[0]
    tile = q_tiles.shape[-1]
    quarters = tile // LANES
    own_x, own_y = primal.shape[0], dual.shape[0]
    wide_h, wide_t = nq * quarters, nk * quarters
    pairs = n_blk // 2
    code_h = sel_h.shape[1] // LANES

    loads = []
    for t in range(nk + nq):
        source = k_tiles.at[t] if t < nk else q_tiles.at[t - nk]
        loads.append(pltpu.make_async_copy(source, raw.at[t], tile_sem.at[t]))
        loads[-1].start()

    barrier = pltpu.get_barrier_semaphore()

    def greet(axis, count, me):
        def body(k, carry):
            pl.semaphore_signal(
                barrier, inc=1, device_id={axis: lax.rem(me + k, count)}, device_id_type=MESH
            )
            return carry

        lax.fori_loop(1, count, body, 0)

    greet("blk", n_blk, blk)
    greet("grp", n_grp, grp)

    def slot(ref, index, size):
        return ref.at[pl.ds(pl.multiple_of(index * size, size), size)]

    q_rows = [q_index[0, p] for p in range(nq)]
    q_cols = [q_index[1, p] for p in range(nq)]
    c_rows = [k_rows[0, p] for p in range(nk)]
    c_cols = [k_cols[0, p] for p in range(nk)]
    code_t = ids_x.shape[1] - code_h
    ids_x[blk, :code_h] = segment(q_rows, blk * wide_h, wide_h, code_h, quarters)
    ids_x[blk, code_h:] = segment(c_cols, blk * wide_t, wide_t, code_t, quarters)
    ids_y[grp] = segment(c_rows, grp * wide_t, wide_t, ids_y.shape[1], quarters)
    kind = bound_kind[...]
    mine_x = pl.ds(pl.multiple_of(blk * own_x, own_x), own_x)
    mine_y = pl.ds(pl.multiple_of(grp * own_y, own_y), own_y)
    data[0, mine_x] = objective[...]
    data[1, mine_x] = jnp.where((kind == 1) | (kind == 2), lower[...], -jnp.inf)
    data[2, mine_x] = jnp.where((kind == 2) | (kind == 3), upper[...], jnp.inf)
    rows_data[0, mine_y] = rhs[...]
    rows_data[1, mine_y] = jnp.where(row_kind[...] == 1, 0.0, -jnp.inf)
    xs[mine_x] = primal[...]
    ys[mine_y] = dual[...]

    pl.semaphore_wait(barrier, n_blk + n_grp - 2)

    leaving = []
    used = {"blk": 0, "grp": 0}

    def share(axis, source, target):
        at = used[axis]
        used[axis] += 1
        count, me = (n_blk, blk) if axis == "blk" else (n_grp, grp)
        send, recv = (blk_send, blk_recv) if axis == "blk" else (grp_send, grp_recv)
        arrive, leave = exchange(
            axis, count, me, source, target, send.at[at], recv.at[at]
        )
        leaving.append(leave)
        return arrive

    y_here = share("grp", dual, lambda s: slot(ys, s, own_y))

    outer, inner = lax.div(blk, 2), lax.rem(blk, 2)

    def passing(view, at, k, theirs, other):
        there = lax.rem(outer + k, pairs) * 2
        if other:
            sent, got, to = there + inner, there + 1 - inner, outer * 2 + 1 - inner
        else:
            sent, got, to = blk, there + inner, there + inner
        return pltpu.make_async_remote_copy(
            src_ref=view(sent),
            dst_ref=view(got if theirs else sent),
            send_sem=blk_send.at[at, k],
            recv_sem=blk_recv.at[at, got if theirs else sent],
            device_id={"blk": to},
            device_id_type=MESH,
        )

    def each(first, call):
        def body(k, carry):
            call(k)
            return carry

        lax.fori_loop(first, pairs, body, 0)

    def begin(view, own, other):
        passing(view, other, 0, False, True).start()
        each(1, lambda k: passing(view, own, k, False, False).start())

    def relay(view, own, other):
        def one(k):
            passing(view, own, k, True, False).wait_recv()
            passing(view, other, k, False, True).start()

        each(1, one)

    def finish(view, own, other):
        each(0, lambda k: passing(view, other, k, True, True).wait_recv())

    def depart(view, own, other):
        each(0, lambda k: passing(view, other, k, False, True).wait_send())
        each(1, lambda k: passing(view, own, k, False, False).wait_send())

    def reserve():
        used["blk"] += 1
        return used["blk"] - 1

    x_view = lambda s: slot(xs, s, own_x)
    x_at = (reserve(), reserve())
    begin(x_view, *x_at)
    ids_y_here = share("grp", ids_y.at[grp], lambda s: ids_y.at[s])
    def planes(ref, index, size):
        return ref.at[:, pl.ds(pl.multiple_of(index * size, size), size)]

    rows_here = share("grp", planes(rows_data, grp, own_y), lambda s: planes(rows_data, s, own_y))
    def unpack(t):
        loads[t].wait()
        whi[t], wlo[t] = split(raw[t])

    row = lax.broadcasted_iota(jnp.int32, (16, tile), 0)

    def product(vector, index, t, transposed):
        piece = jnp.concatenate(
            [vector[pl.ds(index * quarters + q, 1), :] for q in range(quarters)], axis=1
        )
        high = piece.astype(BF16).astype(F32)
        left = jnp.where(row == 0, high, jnp.where(row == 1, piece - high, 0.0)).astype(BF16)
        dims = (((1,), (0 if transposed else 1,)), ((), ()))
        out = lax.dot_general(left, whi[t], dims, preferred_element_type=F32)
        out = out + lax.dot_general(left, wlo[t], dims, preferred_element_type=F32)
        return out[0:1] + out[1:2]

    def put(ref, first, values):
        for q in range(quarters):
            ref[pl.ds(first + q, 1), :] = values[:, q * LANES : (q + 1) * LANES]

    def row_block(ref, step, index, size):
        return ref.at[step, pl.ds(pl.multiple_of(index * size, 8), size)]

    def transposed(step):
        mine = row_block(vals_t, step, blk, wide_t)
        for p in range(nk):
            put(mine, p * quarters, -product(ys, c_rows[p], p, True))
        return share("blk", mine, lambda s: row_block(vals_t, step, s, wide_t))

    def hessian(step):
        mine = row_block(vals_h, step, blk, wide_h)
        for p in range(nq):
            put(mine, p * quarters, product(xs, q_cols[p], nk + p, False))
        return share("blk", mine, lambda s: row_block(vals_h, step, s, wide_h))

    def spread(axis, ref, step, value):
        me = blk if axis == "blk" else grp
        ref[step, me] = jnp.broadcast_to(value, (1, LANES))
        return share(axis, ref.at[step, me], lambda s: ref.at[step, s])

    def constraint(step):
        mine = row_block(vals_y, step, grp, wide_t)
        for p in range(nk):
            fresh = product(xs, c_cols[p], p, False)
            for q in range(quarters):
                part = fresh[:, q * LANES : (q + 1) * LANES]
                at = pl.ds(p * quarters + q, 1)
                mine[at, :] = 2.0 * part - cons_now[at, :]
                cons_now[at, :] = part
        return share("grp", mine, lambda s: row_block(vals_y, step, s, wide_t))

    def parts(values):
        return jnp.concatenate(split(values), axis=1)

    def gathered(*terms):
        both = sum(
            jnp.dot(selector, values, preferred_element_type=F32) for selector, values in terms
        )
        return both[:, :LANES] + both[:, LANES:]

    def scalar_sum(ref, step, count):
        total = ref[step, 0]
        for s in range(1, count):
            total = total + ref[step, s]
        return total

    def full_sum(values):
        return jnp.sum(jnp.sum(values, axis=0, keepdims=True), axis=1, keepdims=True)

    chunk_x = min(CHUNK, n_blk * own_x)
    chunk_y = min(CHUNK, n_grp * own_y)

    def selectors():
        ids_y_here()
        ids_x_here()
        codes_x, codes_y = jnp.sum(ids_x[...], axis=0), jnp.sum(ids_y[...], axis=0)
        for ref, codes, chunk in (
            (sel_h, codes_x[:code_h], chunk_x),
            (sel_t, codes_x[code_h:], chunk_x),
            (sel_y, codes_y, chunk_y),
        ):

            def body(c, carry):
                base = pl.multiple_of(c * chunk, chunk)
                at = lax.broadcasted_iota(jnp.int32, (chunk, LANES), 0) + base
                for k in range(ref.shape[1] // LANES):
                    hit = at == codes[k : k + 1, :]
                    ref[pl.ds(base, chunk), k * LANES : (k + 1) * LANES] = jnp.where(
                        hit, 1.0, 0.0
                    ).astype(BF16)
                return carry

            lax.fori_loop(0, ref.shape[0] // chunk, body, 0)

    def primal_step(step, tau):
        from_h, from_t = parts(vals_h[step]), parts(vals_t[step])

        def body(c, total):
            at = pl.ds(pl.multiple_of(c * chunk_x, chunk_x), chunk_x)
            gradient = gathered(
                (sel_h[at, : n_blk * wide_h], from_h), (sel_t[at, : n_blk * wide_t], from_t)
            )
            gradient = gradient + data[0, at]
            now = xs[at]
            new = jnp.minimum(jnp.maximum(now - tau * gradient, data[1, at]), data[2, at])
            xs[at] = new
            return total + full_sum((new - now) * (new - now))

        return lax.fori_loop(0, n_blk * own_x // chunk_x, body, jnp.zeros((1, 1), F32))

    def dual_step(step, sigma):
        values = parts(vals_y[step])

        def body(c, total):
            at = pl.ds(pl.multiple_of(c * chunk_y, chunk_y), chunk_y)
            extrap = gathered((sel_y[at, : n_grp * wide_t], values))
            now = ys[at]
            new = jnp.maximum(now + sigma * (rows_data[0, at] - extrap), rows_data[1, at])
            ys[at] = new
            return total + full_sum((new - now) * (new - now))

        return lax.fori_loop(0, n_grp * own_y // chunk_y, body, jnp.zeros((1, 1), F32))

    weight = jnp.ones((1, LANES), F32)
    for t in range(nk):
        unpack(t)
    y_here()
    transposed_here = transposed(0)
    ids_x_here = share("blk", ids_x.at[blk], lambda s: ids_x.at[s])
    relay(x_view, *x_at)
    views = []
    for plane in range(data.shape[0]):
        view = functools.partial(lambda plane, s: slot(data.at[plane], s, own_x), plane)
        views.append((view, reserve(), reserve()))
        begin(*views[-1])
    for t in range(nk, nk + nq):
        unpack(t)
    finish(x_view, *x_at)
    hessian_here = hessian(0)
    for p in range(nk):
        put(cons_now, p * quarters, product(xs, c_cols[p], p, False))

    for item in views:
        relay(*item)
    selectors()
    for item in views:
        finish(*item)
    depart(x_view, *x_at)
    for step in range(ITERS):
        hessian_here()
        transposed_here()
        if step > 0:
            dual_here()
            dual_total = scalar_sum(sums_x, step - 1, n_blk)
            weight = jnp.sqrt(
                weight * jnp.sqrt((dual_total + EPSILON) / (primal_total + EPSILON))
            )
        primal_sq = primal_step(step, STEP_SCALE / weight)
        constraint_here = constraint(step)
        primal_here = spread("grp", sums_y, step, primal_sq)
        if step < ITERS - 1:
            hessian_here = hessian(step + 1)
        if step == 0:
            rows_here()
        constraint_here()
        dual_sq = dual_step(step, STEP_SCALE * weight)
        dual_here = spread("blk", sums_x, step, dual_sq)
        if step < ITERS - 1:
            transposed_here = transposed(step + 1)
        primal_here()
        primal_total = scalar_sum(sums_y, step, n_grp)

    x_out[...] = xs[mine_x]
    y_out[...] = ys[mine_y]
    dual_here()
    dual_total = scalar_sum(sums_x, ITERS - 1, n_blk)
    weight = jnp.sqrt(weight * jnp.sqrt((dual_total + EPSILON) / (primal_total + EPSILON)))
    w_out[...] = weight[:, :1]
    for item in views:
        depart(*item)
    for leave in leaving:
        leave()


def up(value, step):
    return -(-value // step) * step


def shards(
    primal,
    dual,
    objective,
    lower,
    upper,
    bound_kind,
    rhs,
    row_kind,
    q_tiles,
    q_index,
    k_tiles,
    k_rows,
    k_cols,
):
    n_blk, n_grp = lax.axis_size("blk"), lax.axis_size("grp")
    nq, nk, tile = q_tiles.shape[1], k_tiles.shape[1], q_tiles.shape[-1]
    quarters = tile // LANES
    own_x, own_y = primal.shape[0] // LANES, dual.shape[0] // LANES
    wide_h, wide_t = nq * quarters, nk * quarters
    code_h, code_t = up(n_blk * wide_h, LANES), up(n_blk * wide_t, LANES)
    code_y = up(n_grp * wide_t, LANES)
    vmem = pl.BlockSpec(memory_space=pltpu.VMEM)
    smem = pl.BlockSpec(memory_space=pltpu.SMEM)
    hbm = pl.BlockSpec(memory_space=pl.ANY)

    def lanes(values):
        return values.reshape(-1, LANES)

    x, y, weight = pl.pallas_call(
        functools.partial(kernel, n_blk, n_grp),
        out_shape=(
            jax.ShapeDtypeStruct((own_x, LANES), F32),
            jax.ShapeDtypeStruct((own_y, LANES), F32),
            jax.ShapeDtypeStruct((1, 1), F32),
        ),
        in_specs=[vmem] * 8 + [smem] * 3 + [hbm] * 2,
        out_specs=(vmem, vmem, vmem),
        scratch_shapes=[
            pltpu.VMEM((nk + nq, tile, tile), F32),
            pltpu.VMEM((nk + nq, tile, tile), BF16),
            pltpu.VMEM((nk + nq, tile, tile), BF16),
            pltpu.VMEM((n_blk * own_x, LANES), F32),
            pltpu.VMEM((n_grp * own_y, LANES), F32),
            pltpu.VMEM((3, n_blk * own_x, LANES), F32),
            pltpu.VMEM((2, n_grp * own_y, LANES), F32),
            pltpu.VMEM((n_blk, (code_h + code_t) // LANES, LANES), jnp.int32),
            pltpu.VMEM((n_grp, code_y // LANES, LANES), jnp.int32),
            pltpu.VMEM((n_blk * own_x, code_h), BF16),
            pltpu.VMEM((n_blk * own_x, code_t), BF16),
            pltpu.VMEM((n_grp * own_y, code_y), BF16),
            pltpu.VMEM((ITERS, n_blk * wide_h, LANES), F32),
            pltpu.VMEM((ITERS, n_blk * wide_t, LANES), F32),
            pltpu.VMEM((ITERS, n_grp * wide_t, LANES), F32),
            pltpu.VMEM((ITERS, n_blk, 1, LANES), F32),
            pltpu.VMEM((ITERS, n_grp, 1, LANES), F32),
            pltpu.VMEM((nk * quarters, LANES), F32),
            pltpu.SemaphoreType.DMA((nk + nq,)),
            pltpu.SemaphoreType.DMA((3 * ITERS + 9, n_blk)),
            pltpu.SemaphoreType.DMA((3 * ITERS + 9, n_blk)),
            pltpu.SemaphoreType.DMA((2 * ITERS + 3, n_grp)),
            pltpu.SemaphoreType.DMA((2 * ITERS + 3, n_grp)),
        ],
        compiler_params=pltpu.CompilerParams(
            collective_id=0, has_side_effects=True, vmem_limit_bytes=60 * 1024 * 1024
        ),
    )(
        lanes(primal),
        lanes(dual),
        lanes(objective),
        lanes(lower),
        lanes(upper),
        lanes(bound_kind),
        lanes(rhs),
        lanes(row_kind),
        q_index[0],
        k_rows,
        k_cols,
        q_tiles[0],
        k_tiles[0],
    )
    return x.reshape(-1), y.reshape(-1), weight.reshape(())


def solution(mesh):
    vector = P(("blk", "grp"))
    return jax.shard_map(
        shards,
        mesh=mesh,
        in_specs=(vector,) * 8
        + (
            P("grp", "blk", None, None),
            P("grp", None, "blk"),
            P("grp", "blk", None, None),
            P("grp", "blk"),
            P("grp", "blk"),
        ),
        out_specs=(vector, vector, P()),
        check_vma=False,
    )
```

profile of v0, /device:TPU:0, one launch (start us, length us, event | category | flops | bytes accessed | tf_op | source)
XLA Modules:
  0.0 57.7 jit_solution(8447815944668886957)
XLA Ops:
  0.6 52.6 %shard_map.148 = (f32[64,128]{1,0:T(8,128)}, f32[32,128]{1,0:T(8,128)}, f32[1,1]{1,0:T(1,128)}) custom-call(f32[64,128]{1,0:T(8,128)} %bitcast.16, f32[32,128]{1,0:T(8,128)} %bitcast.22, f32[64,128]{1,0:T(8,128)} %bitcast.17, f32[64,128]{1,0:T(8,128)} %bitcast.18, f32[64,128]{1,0:T(8,128)} %bitcast.19, s32[64,128]{1,0:T(8,128)} %bitcast.20, ...), custom_call_target="tpu_custom_call" | custom-call | tf_op jit(solution)/shard_map/pallas_call | solution.py:450
  53.3 1.4 %copy.19 = f32[8192]{0:T(1024)} copy(f32[8192]{0:T(1024)} %bitcast.21) | data formatting | bytes 65536
  54.7 1.3 %copy.20 = f32[4096]{0:T(1024)} copy(f32[4096]{0:T(1024)} %bitcast.25) | data formatting | bytes 32768
where the time goes:
time: 58.1 us; the launch traced here: 57.7 us
  Pallas kernels  52.6 us (91%)
  local copies, waits for them, and re-layouts  2.7 us (5%)
  between operations  2.38 us (4%)
    pallas_call x1, Pallas kernels, shards(): pl.pallas_call(functools.partial(kernel, n_blk, n_grp), out_shape=(jax.Sh...  52.6 us
    unnamed x2, local copies, waits for them, and re-layouts  2.7 us

commit v1 on v0

--- a/solution.py
+++ b/solution.py
@@ -22,34 +22,23 @@
     return high, (values - high.astype(F32)).astype(BF16)
 
 
-def exchange(axis, count, me, source, target, send, recv):
-    def copy(k, slot):
-        peer = lax.rem(me + k, count)
-        return pltpu.make_async_remote_copy(
+def exchange(axis, count, me, source, target, others, send, recv):
+    def start(k, carry):
+        peer = lax.rem(me + count - k, count)
+        pltpu.make_async_remote_copy(
             src_ref=source,
-            dst_ref=target(me if slot else peer),
-            send_sem=send.at[k],
-            recv_sem=recv.at[me if slot else peer],
+            dst_ref=target(me),
+            send_sem=send,
+            recv_sem=recv,
             device_id={axis: peer},
             device_id_type=MESH,
-        )
-
-    def start(k, carry):
-        copy(k, True).start()
-        return carry
-
-    def arrive(k, carry):
-        copy(k, False).wait_recv()
-        return carry
-
-    def leave(k, carry):
-        copy(k, True).wait_send()
+        ).start()
         return carry
 
     lax.fori_loop(1, count, start, 0)
     return (
-        lambda: lax.fori_loop(1, count, arrive, 0),
-        lambda: lax.fori_loop(1, count, leave, 0),
+        lambda: pltpu.make_async_copy(others, others, recv).wait(),
+        lambda: pltpu.make_async_copy(others, others, send).wait(),
     )
 
 
@@ -83,8 +72,13 @@
     y_out,
     w_out,
     raw,
-    whi,
-    wlo,
+    staged,
+    kinds,
+    staged_rows,
+    weight_out,
+    q_at,
+    r_at,
+    c_at,
     xs,
     ys,
     data,
@@ -101,8 +95,11 @@
     sums_y,
     cons_now,
     tile_sem,
+    io_sem,
     blk_send,
     blk_recv,
+    one_send,
+    one_recv,
     grp_send,
     grp_recv,
 ):
@@ -115,12 +112,6 @@
     pairs = n_blk // 2
     code_h = sel_h.shape[1] // LANES
 
-    loads = []
-    for t in range(nk + nq):
-        source = k_tiles.at[t] if t < nk else q_tiles.at[t - nk]
-        loads.append(pltpu.make_async_copy(source, raw.at[t], tile_sem.at[t]))
-        loads[-1].start()
-
     barrier = pltpu.get_barrier_semaphore()
 
     def greet(axis, count, me):
@@ -135,45 +126,65 @@
     greet("blk", n_blk, blk)
     greet("grp", n_grp, grp)
 
+    mine_x = pl.ds(pl.multiple_of(blk * own_x, own_x), own_x)
+    mine_y = pl.ds(pl.multiple_of(grp * own_y, own_y), own_y)
+    fetched = []
+    for source, target in (
+        (dual, ys.at[mine_y]),
+        (primal, xs.at[mine_x]),
+        (q_index, q_at),
+        (k_rows, r_at),
+        (k_cols, c_at),
+        (objective, data.at[0, mine_x]),
+        (lower, staged.at[0]),
+        (upper, staged.at[1]),
+        (bound_kind, kinds),
+        (rhs, rows_data.at[0, mine_y]),
+        (row_kind, staged_rows),
+    ):
+        fetched.append(pltpu.make_async_copy(source, target, io_sem.at[len(fetched)]))
+        fetched[-1].start()
+    for item in fetched:
+        item.wait()
+    loads = []
+    for t in range(nk + nq):
+        source = k_tiles.at[t] if t < nk else q_tiles.at[t - nk]
+        loads.append(pltpu.make_async_copy(source, raw.at[t], tile_sem.at[t]))
+        loads[-1].start()
+
     def slot(ref, index, size):
         return ref.at[pl.ds(pl.multiple_of(index * size, size), size)]
 
-    q_rows = [q_index[0, p] for p in range(nq)]
-    q_cols = [q_index[1, p] for p in range(nq)]
-    c_rows = [k_rows[0, p] for p in range(nk)]
-    c_cols = [k_cols[0, p] for p in range(nk)]
+    q_rows = [q_at[0, p] for p in range(nq)]
+    q_cols = [q_at[1, p] for p in range(nq)]
+    c_rows = [r_at[0, p] for p in range(nk)]
+    c_cols = [c_at[0, p] for p in range(nk)]
     code_t = ids_x.shape[1] - code_h
     ids_x[blk, :code_h] = segment(q_rows, blk * wide_h, wide_h, code_h, quarters)
     ids_x[blk, code_h:] = segment(c_cols, blk * wide_t, wide_t, code_t, quarters)
     ids_y[grp] = segment(c_rows, grp * wide_t, wide_t, ids_y.shape[1], quarters)
-    kind = bound_kind[...]
-    mine_x = pl.ds(pl.multiple_of(blk * own_x, own_x), own_x)
-    mine_y = pl.ds(pl.multiple_of(grp * own_y, own_y), own_y)
-    data[0, mine_x] = objective[...]
-    data[1, mine_x] = jnp.where((kind == 1) | (kind == 2), lower[...], -jnp.inf)
-    data[2, mine_x] = jnp.where((kind == 2) | (kind == 3), upper[...], jnp.inf)
-    rows_data[0, mine_y] = rhs[...]
-    rows_data[1, mine_y] = jnp.where(row_kind[...] == 1, 0.0, -jnp.inf)
-    xs[mine_x] = primal[...]
-    ys[mine_y] = dual[...]
+    kind = kinds[...]
+    data[1, mine_x] = jnp.where((kind == 1) | (kind == 2), staged[0], -jnp.inf)
+    data[2, mine_x] = jnp.where((kind == 2) | (kind == 3), staged[1], jnp.inf)
+    rows_data[1, mine_y] = jnp.where(staged_rows[...] == 1, 0.0, -jnp.inf)
 
     pl.semaphore_wait(barrier, n_blk + n_grp - 2)
 
     leaving = []
-    used = {"blk": 0, "grp": 0}
-
-    def share(axis, source, target):
+    used = {"blk": 0, "grp": 0, "two": 0}
+
+    def share(axis, source, target, others):
         at = used[axis]
         used[axis] += 1
         count, me = (n_blk, blk) if axis == "blk" else (n_grp, grp)
-        send, recv = (blk_send, blk_recv) if axis == "blk" else (grp_send, grp_recv)
+        send, recv = (one_send, one_recv) if axis == "blk" else (grp_send, grp_recv)
         arrive, leave = exchange(
-            axis, count, me, source, target, send.at[at], recv.at[at]
+            axis, count, me, source, target, others, send.at[at], recv.at[at]
         )
         leaving.append(leave)
         return arrive
 
-    y_here = share("grp", dual, lambda s: slot(ys, s, own_y))
+    y_here = share("grp", ys.at[mine_y], lambda s: slot(ys, s, own_y), ys.at[: (n_grp - 1) * own_y])
 
     outer, inner = lax.div(blk, 2), lax.rem(blk, 2)
 
@@ -218,37 +229,48 @@
         each(1, lambda k: passing(view, own, k, False, False).wait_send())
 
     def reserve():
-        used["blk"] += 1
-        return used["blk"] - 1
+        used["two"] += 1
+        return used["two"] - 1
 
     x_view = lambda s: slot(xs, s, own_x)
     x_at = (reserve(), reserve())
     begin(x_view, *x_at)
-    ids_y_here = share("grp", ids_y.at[grp], lambda s: ids_y.at[s])
+    ids_y_here = share("grp", ids_y.at[grp], lambda s: ids_y.at[s], ids_y.at[: n_grp - 1])
     def planes(ref, index, size):
         return ref.at[:, pl.ds(pl.multiple_of(index * size, size), size)]
 
-    rows_here = share("grp", planes(rows_data, grp, own_y), lambda s: planes(rows_data, s, own_y))
-    def unpack(t):
-        loads[t].wait()
-        whi[t], wlo[t] = split(raw[t])
-
-    row = lax.broadcasted_iota(jnp.int32, (16, tile), 0)
+    rows_here = share("grp", planes(rows_data, grp, own_y), lambda s: planes(rows_data, s, own_y), rows_data.at[:, : (n_grp - 1) * own_y])
+
+    def folded(values):
+        return jnp.sum(values.reshape(-1, 8, LANES), axis=0)
+
+    def strip(vector, index, q):
+        row = vector[pl.ds(index * quarters + q, 1), :]
+        return jnp.broadcast_to(row, (LANES, LANES))
+
+    def block(t, q, c):
+        return raw[t, q * LANES : (q + 1) * LANES, c * LANES : (c + 1) * LANES]
 
     def product(vector, index, t, transposed):
-        piece = jnp.concatenate(
-            [vector[pl.ds(index * quarters + q, 1), :] for q in range(quarters)], axis=1
-        )
-        high = piece.astype(BF16).astype(F32)
-        left = jnp.where(row == 0, high, jnp.where(row == 1, piece - high, 0.0)).astype(BF16)
-        dims = (((1,), (0 if transposed else 1,)), ((), ()))
-        out = lax.dot_general(left, whi[t], dims, preferred_element_type=F32)
-        out = out + lax.dot_general(left, wlo[t], dims, preferred_element_type=F32)
-        return out[0:1] + out[1:2]
+        if transposed:
+            total = [jnp.zeros((8, LANES), F32)] * quarters
+            for q in range(quarters):
+                column = strip(vector, index, q).T
+                for c in range(quarters):
+                    total[c] = total[c] + folded(block(t, q, c) * column)
+        else:
+            rows = [strip(vector, index, c) for c in range(quarters)]
+            total = []
+            for q in range(quarters):
+                part = block(t, q, 0) * rows[0]
+                for c in range(1, quarters):
+                    part = part + block(t, q, c) * rows[c]
+                total.append(folded(part.T))
+        return [jnp.sum(part, axis=0, keepdims=True) for part in total]
 
     def put(ref, first, values):
         for q in range(quarters):
-            ref[pl.ds(first + q, 1), :] = values[:, q * LANES : (q + 1) * LANES]
+            ref[pl.ds(first + q, 1), :] = values[q]
 
     def row_block(ref, step, index, size):
         return ref.at[step, pl.ds(pl.multiple_of(index * size, 8), size)]
@@ -256,30 +278,31 @@
     def transposed(step):
         mine = row_block(vals_t, step, blk, wide_t)
         for p in range(nk):
-            put(mine, p * quarters, -product(ys, c_rows[p], p, True))
-        return share("blk", mine, lambda s: row_block(vals_t, step, s, wide_t))
+            put(mine, p * quarters, [-part for part in product(ys, c_rows[p], p, True)])
+        return share("blk", mine, lambda s: row_block(vals_t, step, s, wide_t), vals_t.at[step, : (n_blk - 1) * wide_t])
 
     def hessian(step):
         mine = row_block(vals_h, step, blk, wide_h)
         for p in range(nq):
             put(mine, p * quarters, product(xs, q_cols[p], nk + p, False))
-        return share("blk", mine, lambda s: row_block(vals_h, step, s, wide_h))
+        return share("blk", mine, lambda s: row_block(vals_h, step, s, wide_h), vals_h.at[step, : (n_blk - 1) * wide_h])
 
     def spread(axis, ref, step, value):
         me = blk if axis == "blk" else grp
         ref[step, me] = jnp.broadcast_to(value, (1, LANES))
-        return share(axis, ref.at[step, me], lambda s: ref.at[step, s])
+        count = n_blk if axis == "blk" else n_grp
+        return share(axis, ref.at[step, me], lambda s: ref.at[step, s], ref.at[step, : count - 1])
 
     def constraint(step):
         mine = row_block(vals_y, step, grp, wide_t)
         for p in range(nk):
             fresh = product(xs, c_cols[p], p, False)
             for q in range(quarters):
-                part = fresh[:, q * LANES : (q + 1) * LANES]
+                part = fresh[q]
                 at = pl.ds(p * quarters + q, 1)
                 mine[at, :] = 2.0 * part - cons_now[at, :]
                 cons_now[at, :] = part
-        return share("grp", mine, lambda s: row_block(vals_y, step, s, wide_t))
+        return share("grp", mine, lambda s: row_block(vals_y, step, s, wide_t), vals_y.at[step, : (n_grp - 1) * wide_t])
 
     def parts(values):
         return jnp.concatenate(split(values), axis=1)
@@ -355,10 +378,10 @@
 
     weight = jnp.ones((1, LANES), F32)
     for t in range(nk):
-        unpack(t)
+        loads[t].wait()
     y_here()
     transposed_here = transposed(0)
-    ids_x_here = share("blk", ids_x.at[blk], lambda s: ids_x.at[s])
+    ids_x_here = share("blk", ids_x.at[blk], lambda s: ids_x.at[s], ids_x.at[: n_blk - 1])
     relay(x_view, *x_at)
     views = []
     for plane in range(data.shape[0]):
@@ -366,12 +389,11 @@
         views.append((view, reserve(), reserve()))
         begin(*views[-1])
     for t in range(nk, nk + nq):
-        unpack(t)
+        loads[t].wait()
     finish(x_view, *x_at)
     hessian_here = hessian(0)
     for p in range(nk):
         put(cons_now, p * quarters, product(xs, c_cols[p], p, False))
-
     for item in views:
         relay(*item)
     selectors()
@@ -389,11 +411,15 @@
             )
         primal_sq = primal_step(step, STEP_SCALE / weight)
         constraint_here = constraint(step)
+        if step == ITERS - 1:
+            x_done = pltpu.make_async_copy(xs.at[mine_x], x_out, io_sem.at[0])
+            x_done.start()
         primal_here = spread("grp", sums_y, step, primal_sq)
         if step < ITERS - 1:
             hessian_here = hessian(step + 1)
         if step == 0:
             rows_here()
+            leaving.pop(0)()
         constraint_here()
         dual_sq = dual_step(step, STEP_SCALE * weight)
         dual_here = spread("blk", sums_x, step, dual_sq)
@@ -401,13 +427,16 @@
             transposed_here = transposed(step + 1)
         primal_here()
         primal_total = scalar_sum(sums_y, step, n_grp)
-
-    x_out[...] = xs[mine_x]
-    y_out[...] = ys[mine_y]
+    y_done = pltpu.make_async_copy(ys.at[mine_y], y_out, io_sem.at[1])
+    y_done.start()
     dual_here()
     dual_total = scalar_sum(sums_x, ITERS - 1, n_blk)
     weight = jnp.sqrt(weight * jnp.sqrt((dual_total + EPSILON) / (primal_total + EPSILON)))
-    w_out[...] = weight[:, :1]
+    weight_out[...] = weight[:, :1]
+    w_done = pltpu.make_async_copy(weight_out, w_out, io_sem.at[2])
+    w_done.start()
+    for item in (x_done, y_done, w_done):
+        item.wait()
     for item in views:
         depart(*item)
     for leave in leaving:
@@ -440,8 +469,6 @@
     wide_h, wide_t = nq * quarters, nk * quarters
     code_h, code_t = up(n_blk * wide_h, LANES), up(n_blk * wide_t, LANES)
     code_y = up(n_grp * wide_t, LANES)
-    vmem = pl.BlockSpec(memory_space=pltpu.VMEM)
-    smem = pl.BlockSpec(memory_space=pltpu.SMEM)
     hbm = pl.BlockSpec(memory_space=pl.ANY)
 
     def lanes(values):
@@ -454,12 +481,17 @@
             jax.ShapeDtypeStruct((own_y, LANES), F32),
             jax.ShapeDtypeStruct((1, 1), F32),
         ),
-        in_specs=[vmem] * 8 + [smem] * 3 + [hbm] * 2,
-        out_specs=(vmem, vmem, vmem),
+        in_specs=[hbm] * 13,
+        out_specs=(hbm, hbm, hbm),
         scratch_shapes=[
             pltpu.VMEM((nk + nq, tile, tile), F32),
-            pltpu.VMEM((nk + nq, tile, tile), BF16),
-            pltpu.VMEM((nk + nq, tile, tile), BF16),
+            pltpu.VMEM((2, own_x, LANES), F32),
+            pltpu.VMEM((own_x, LANES), jnp.int32),
+            pltpu.VMEM((own_y, LANES), jnp.int32),
+            pltpu.VMEM((1, 1), F32),
+            pltpu.SMEM((2, nq), jnp.int32),
+            pltpu.SMEM((1, nk), jnp.int32),
+            pltpu.SMEM((1, nk), jnp.int32),
             pltpu.VMEM((n_blk * own_x, LANES), F32),
             pltpu.VMEM((n_grp * own_y, LANES), F32),
             pltpu.VMEM((3, n_blk * own_x, LANES), F32),
@@ -476,10 +508,13 @@
             pltpu.VMEM((ITERS, n_grp, 1, LANES), F32),
             pltpu.VMEM((nk * quarters, LANES), F32),
             pltpu.SemaphoreType.DMA((nk + nq,)),
-            pltpu.SemaphoreType.DMA((3 * ITERS + 9, n_blk)),
-            pltpu.SemaphoreType.DMA((3 * ITERS + 9, n_blk)),
-            pltpu.SemaphoreType.DMA((2 * ITERS + 3, n_grp)),
-            pltpu.SemaphoreType.DMA((2 * ITERS + 3, n_grp)),
+            pltpu.SemaphoreType.DMA((11,)),
+            pltpu.SemaphoreType.DMA((8, n_blk)),
+            pltpu.SemaphoreType.DMA((8, n_blk)),
+            pltpu.SemaphoreType.DMA((3 * ITERS + 1,)),
+            pltpu.SemaphoreType.DMA((3 * ITERS + 1,)),
+            pltpu.SemaphoreType.DMA((2 * ITERS + 3,)),
+            pltpu.SemaphoreType.DMA((2 * ITERS + 3,)),
         ],
         compiler_params=pltpu.CompilerParams(
             collective_id=0, has_side_effects=True, vmem_limit_bytes=60 * 1024 * 1024

time: 58.1 us -> 51.3 us (0.88)
  Pallas kernels: 52.6 us -> 45.8 us
    pallas_call x1, Pallas kernels: 52.6 us -> 45.8 us  [shards(): pl.pallas_call(functools.partial(kernel, n_blk, n_grp), out_shape=(jax.Sh...]
where the time goes in v1:
time: 51.3 us; the launch traced here: 50.9 us
  Pallas kernels  45.8 us (89%)
  local copies, waits for them, and re-layouts  2.7 us (5%)
  between operations  2.38 us (5%)
    pallas_call x1, Pallas kernels, shards(): pl.pallas_call(functools.partial(kernel, n_blk, n_grp), out_shape=(jax.Sh...  45.8 us
    unnamed x2, local copies, waits for them, and re-layouts  2.7 us

profile of v1, /device:TPU:0, one launch (start us, length us, event | category | flops | bytes accessed | tf_op | source)
XLA Modules:
  0.0 50.9 jit_solution(2451112078603254603)
XLA Ops:
  0.6 45.8 %shard_map.148 = (f32[64,128]{1,0:T(8,128)}, f32[32,128]{1,0:T(8,128)}, f32[1,1]{1,0:T(1,128)}) custom-call(f32[64,128]{1,0:T(8,128)} %bitcast.16, f32[32,128]{1,0:T(8,128)} %bitcast.22, f32[64,128]{1,0:T(8,128)} %bitcast.17, f32[64,128]{1,0:T(8,128)} %bitcast.18, f32[64,128]{1,0:T(8,128)} %bitcast.19, s32[64,128]{1,0:T(8,128)} %bitcast.20, ...), custom_call_target="tpu_custom_call" | custom-call | tf_op jit(solution)/shard_map/pallas_call | solution.py:477
  46.5 1.4 %copy.19 = f32[8192]{0:T(1024)} copy(f32[8192]{0:T(1024)} %bitcast.21) | data formatting | bytes 65536
  47.8 1.3 %copy.20 = f32[4096]{0:T(1024)} copy(f32[4096]{0:T(1024)} %bitcast.25) | data formatting | bytes 32768

commit v2 on v1

v2 whole, which is shorter than its diff:
```python
import functools

import jax
import jax.numpy as jnp
from jax import lax
from jax.experimental import pallas as pl
from jax.experimental.pallas import tpu as pltpu
from jax.sharding import PartitionSpec as P

ITERS = 2
EPSILON = 1e-06
STEP_SCALE = 0.5
LANES = 128
UNROLL = 8
FREE = 2.0**100
MESH = pl.DeviceIdType.MESH
F32 = jnp.float32
BF16 = jnp.bfloat16


def up(value, step):
    return -(-value // step) * step


def split(values, count=2):
    parts = []
    for _ in range(count):
        parts.append(values.astype(BF16))
        values = values - parts[-1].astype(F32)
    return parts


def partner(me, k, count):
    if count & (count - 1):
        return lax.rem(me + k, count)
    result = 0
    bit = 1
    while bit < count:
        mine, theirs = lax.rem(lax.div(me, bit), 2), lax.rem(lax.div(jnp.int32(k), bit), 2)
        result = result + lax.rem(mine + theirs, 2) * bit
        bit *= 2
    return result


def repeat(first, count, call):
    if count <= UNROLL:
        for k in range(first, count):
            call(k)
    else:

        def body(k, carry):
            call(k)
            return carry

        lax.fori_loop(first, count, body, 0)


def segment(ids, start, width, rows, quarters):
    place = lax.broadcasted_iota(jnp.int32, (rows, LANES), 0) * LANES
    place = place + lax.broadcasted_iota(jnp.int32, (rows, LANES), 1) - start
    result = jnp.full((rows, LANES), -1, jnp.int32)
    for p, tile_id in enumerate(ids):
        for q in range(quarters):
            result = jnp.where(place == p * quarters + q, tile_id * quarters + q, result)
    return jnp.where((place >= 0) & (place < width), result, 0)


def kernel(
    n_blk,
    n_grp,
    primal,
    dual,
    objective,
    lower,
    upper,
    bound_kind,
    rhs,
    row_kind,
    q_index,
    k_rows,
    k_cols,
    q_tiles,
    k_tiles,
    x_out,
    y_out,
    w_out,
    raw,
    kinds,
    row_kinds,
    weight_out,
    q_at,
    r_at,
    c_at,
    xs,
    ys,
    xw,
    both,
    data,
    rows_data,
    slot_out,
    slot_in,
    ids_x,
    ids_y,
    sel_h,
    sel_t,
    sel_y,
    vals_h,
    vals_t,
    vals_y,
    sums_x,
    sums_y,
    cons_now,
    tile_sem,
    io_sem,
    far_recv,
    one_send,
    one_recv,
    blk_send,
    blk_recv,
    grp_send,
    grp_recv,
):
    blk, grp = lax.axis_index("blk"), lax.axis_index("grp")
    nq, nk = q_tiles.shape[0], k_tiles.shape[0]
    quarters = q_tiles.shape[-1] // LANES
    own_x, own_y = primal.shape[0], dual.shape[0]
    wide_h, wide_t = nq * quarters, nk * quarters
    pairs = n_blk // 2
    outer, inner = lax.div(blk, 2), lax.rem(blk, 2)
    beside = outer * 2 + 1 - inner
    code_h, code_t = sel_h.shape[1] // LANES, sel_t.shape[1] // LANES
    q_first = up(wide_t, 16)
    first_k, first_q = own_x, own_x + q_first
    last = first_q + wide_h

    barrier = pltpu.get_barrier_semaphore()

    def greet(axis, count, me):
        def one(k):
            pl.semaphore_signal(
                barrier,
                inc=1,
                device_id={axis: partner(me, k, count)},
                device_id_type=MESH,
            )

        repeat(1, count, one)

    greet("blk", n_blk, blk)
    greet("grp", n_grp, grp)

    def part(index, size):
        return pl.ds(pl.multiple_of(index * size, size), size)

    fetched = []
    mine_pair = part(inner, own_x)
    for at, (source, target) in enumerate(
        (
            (dual, ys.at[part(grp, own_y)]),
            (primal, xs.at[part(blk, own_x)]),
            (q_index, q_at),
            (k_rows, r_at),
            (k_cols, c_at),
            (bound_kind, kinds),
            (rhs, rows_data.at[0, part(grp, own_y)]),
            (row_kind, row_kinds),
            (objective, both.at[0, mine_pair]),
            (lower, both.at[1, mine_pair]),
            (upper, both.at[2, mine_pair]),
        )
    ):
        fetched.append(pltpu.make_async_copy(source, target, io_sem.at[at]))
        fetched[-1].start()
    for item in fetched:
        item.wait()
    for t in range(nk):
        pltpu.make_async_copy(k_tiles.at[t], raw.at[t], tile_sem.at[0]).start()
    for t in range(nq):
        pltpu.make_async_copy(q_tiles.at[t], raw.at[nk + t], tile_sem.at[1]).start()

    q_rows = [q_at[0, p] for p in range(nq)]
    q_cols = [q_at[1, p] for p in range(nq)]
    c_rows = [r_at[0, p] for p in range(nk)]
    c_cols = [c_at[0, p] for p in range(nk)]
    ids_x[blk, :code_h] = segment(q_rows, blk * wide_h, wide_h, code_h, quarters)
    ids_x[blk, code_h : code_h + code_t] = segment(
        c_cols, blk * wide_t, wide_t, code_t, quarters
    )
    wanted = c_cols + [-1] * ((q_first - wide_t) // quarters) + q_cols
    ids_x[blk, code_h + code_t :] = segment(
        wanted, 0, q_first + wide_h, ids_x.shape[1] - code_h - code_t, quarters
    )
    ids_y[grp] = segment(c_rows, grp * wide_t, wide_t, ids_y.shape[1], quarters)
    kind = kinds[...]
    both[1, mine_pair] = jnp.where((kind == 1) | (kind == 2), both[1, mine_pair], -FREE)
    both[2, mine_pair] = jnp.where((kind == 2) | (kind == 3), both[2, mine_pair], FREE)
    rows_data[1, part(grp, own_y)] = jnp.where(row_kinds[...] == 1, 0.0, -FREE)

    pl.semaphore_wait(barrier, n_blk + n_grp - 2)

    leaving = []
    used = {"blk": 0, "grp": 0, "one": 0}

    def waiter(ref, sem):
        return lambda: pltpu.make_async_copy(ref, ref, sem).wait()

    def send(axis, peer, source, target, send_sem, recv_sem):
        pltpu.make_async_remote_copy(
            src_ref=source,
            dst_ref=target,
            send_sem=send_sem,
            recv_sem=recv_sem,
            device_id={axis: peer},
            device_id_type=MESH,
        ).start()

    def share(axis, mine, others):
        at = used[axis]
        used[axis] += 1
        count, me = (n_blk, blk) if axis == "blk" else (n_grp, grp)
        sends, recvs = (blk_send, blk_recv) if axis == "blk" else (grp_send, grp_recv)
        repeat(
            1,
            count,
            lambda k: send(
                axis, partner(me, count - k, count), mine, mine, sends.at[at], recvs.at[at]
            ),
        )
        leaving.append(waiter(others, sends.at[at]))
        return waiter(others, recvs.at[at])

    def single():
        used["one"] += 1
        return one_send.at[used["one"] - 1], one_recv.at[used["one"] - 1]

    y_here = share("grp", ys.at[part(grp, own_y)], ys.at[: (n_grp - 1) * own_y])
    ids_x_here = share("blk", ids_x.at[blk], ids_x.at[: n_blk - 1])

    far_send = single()[0]
    near_send, near_recv = single()

    def x_slot(s):
        return xs.at[part(s, own_x)]

    def x_far(k):
        send(
            "blk",
            partner(outer, pairs - k, pairs) * 2 + inner,
            x_slot(blk),
            x_slot(blk),
            far_send,
            far_recv.at[outer],
        )

    def x_relay(k):
        there = partner(outer, k, pairs)
        source = x_slot(there * 2 + inner)
        waiter(source, far_recv.at[there])()
        send("blk", beside, source, source, near_send, near_recv)

    repeat(1, pairs, x_far)
    send("blk", beside, x_slot(blk), x_slot(blk), near_send, near_recv)
    x_here = waiter(xs.at[: pairs * own_x], near_recv)
    leaving.append(waiter(xs.at[: (pairs - 1) * own_x], far_send))
    leaving.append(waiter(xs.at[: pairs * own_x], near_send))

    planes_send, planes_recv = single()
    planes = both.at[:, mine_pair]
    send("blk", beside, planes, planes, planes_send, planes_recv)
    planes_here = waiter(planes, planes_recv)
    leaving.append(waiter(planes, planes_send))

    ids_y_here = share("grp", ids_y.at[grp], ids_y.at[: n_grp - 1])
    rows_here = share(
        "grp", rows_data.at[:, part(grp, own_y)], rows_data.at[:, : (n_grp - 1) * own_y]
    )

    xw[:own_x] = xs[part(blk, own_x)]
    data[:, :own_x] = both[:, mine_pair]
    xw[first_k + wide_t : first_q] = jnp.zeros((q_first - wide_t, LANES), F32)
    data[:, first_k + wide_t : first_q] = jnp.zeros((3, q_first - wide_t, LANES), F32)

    def folded(values):
        return jnp.sum(values.reshape(-1, 8, LANES), axis=0)

    def strip(vector, first, q):
        return jnp.broadcast_to(vector[pl.ds(first + q, 1), :], (LANES, LANES))

    def block(t, q, c):
        return raw[t, q * LANES : (q + 1) * LANES, c * LANES : (c + 1) * LANES]

    def product(vector, first, t, transposed):
        if transposed:
            total = [jnp.zeros((8, LANES), F32)] * quarters
            for q in range(quarters):
                column = strip(vector, first, q).T
                for c in range(quarters):
                    total[c] = total[c] + folded(block(t, q, c) * column)
        else:
            rows = [strip(vector, first, c) for c in range(quarters)]
            total = []
            for q in range(quarters):
                piece = block(t, q, 0) * rows[0]
                for c in range(1, quarters):
                    piece = piece + block(t, q, c) * rows[c]
                total.append(folded(piece.T))
        return [jnp.sum(piece, axis=0, keepdims=True) for piece in total]

    def row_block(ref, step, index, size):
        return ref.at[step, pl.ds(pl.multiple_of(index * size, 8), size)]

    def transposed(step):
        mine = row_block(vals_t, step, blk, wide_t)
        for p in range(nk):
            for q, piece in enumerate(product(ys, c_rows[p] * quarters, p, True)):
                mine[pl.ds(p * quarters + q, 1), :] = -piece
        return share("blk", mine, vals_t.at[step, : (n_blk - 1) * wide_t])

    def hessian(step):
        mine = row_block(vals_h, step, blk, wide_h)
        for p in range(nq):
            for q, piece in enumerate(product(xw, first_q + p * quarters, nk + p, False)):
                mine[pl.ds(p * quarters + q, 1), :] = piece
        return share("blk", mine, vals_h.at[step, : (n_blk - 1) * wide_h])

    def constraint_now(call):
        for p in range(nk):
            for q, piece in enumerate(product(xw, first_k + p * quarters, p, False)):
                call(pl.ds(p * quarters + q, 1), piece)

    def constraint(step):
        mine = row_block(vals_y, step, grp, wide_t)

        def put(at, piece):
            mine[at, :] = 2.0 * piece - cons_now[at, :]
            if step < ITERS - 1:
                cons_now[at, :] = piece

        constraint_now(put)
        return share("grp", mine, vals_y.at[step, : (n_grp - 1) * wide_t])

    def spread(axis, ref, step, value):
        me, count = (blk, n_blk) if axis == "blk" else (grp, n_grp)
        ref[step, me] = jnp.broadcast_to(value, (1, LANES))
        return share(axis, ref.at[step, me], ref.at[step, : count - 1])

    def parts(values):
        return jnp.concatenate(split(values), axis=1)

    def gathered(*terms):
        total = sum(
            jnp.dot(selector, values, preferred_element_type=F32) for selector, values in terms
        )
        return total[:, :LANES] + total[:, LANES:]

    def scalar_sum(ref, step, count):
        total = ref[step, 0]
        for s in range(1, count):
            total = total + ref[step, s]
        return total

    def full_sum(values):
        return jnp.sum(jnp.sum(values, axis=0, keepdims=True), axis=1, keepdims=True)

    def selector(ref, place, codes):
        for k in range(ref.shape[1] // LANES):
            ref[:, k * LANES : (k + 1) * LANES] = jnp.where(
                place == codes[k : k + 1, :], 1.0, 0.0
            ).astype(BF16)

    def selectors():
        ids_y_here()
        codes = jnp.sum(ids_x[:, : code_h + code_t], axis=0)
        line = lax.broadcasted_iota(jnp.int32, (last, LANES), 0)
        place = jnp.where(line < own_x, line + blk * own_x, -1)
        for ids, first in ((c_cols, first_k), (q_cols, first_q)):
            for p, tile_id in enumerate(ids):
                begin = first + p * quarters
                inside = (line >= begin) & (line < begin + quarters)
                place = jnp.where(inside, line - begin + tile_id * quarters, place)
        selector(sel_h, place, codes[:code_h])
        selector(sel_t, place, codes[code_h:])
        line = lax.broadcasted_iota(jnp.int32, (sel_y.shape[0], LANES), 0)
        selector(sel_y, line, jnp.sum(ids_y[...], axis=0))

    def picked():
        values = jnp.concatenate(
            [piece for plane in range(3) for piece in split(both[plane], 3)], axis=1
        )
        line = lax.broadcasted_iota(jnp.int32, (2 * own_x, LANES), 0) + outer * (2 * own_x)

        def one(k):
            there = partner(outer, k, pairs)
            codes = ids_x[there * 2 + inner, code_h + code_t :]
            hits = jnp.where(line == codes, 1.0, 0.0).T[: slot_out.shape[2]].astype(BF16)
            taken = jnp.dot(hits, values, preferred_element_type=F32)
            for plane in range(3):
                pieces = [
                    taken[:, (plane * 3 + i) * LANES : (plane * 3 + i + 1) * LANES]
                    for i in range(3)
                ]
                slot_out[there, plane] = pieces[0] + (pieces[1] + pieces[2])

        repeat(0, pairs, one)

    def hand_out(first, width):
        send_sem, recv_sem = single()

        def one(k):
            there = partner(outer, pairs - k, pairs)
            send(
                "blk",
                there * 2 + inner,
                slot_out.at[there, :, first : first + width],
                slot_in.at[outer, :, first : first + width],
                send_sem,
                recv_sem,
            )

        repeat(1, pairs, one)
        whole = slot_in.at[: pairs - 1, :, first : first + width]
        leaving.append(waiter(whole, send_sem))
        here = waiter(whole, recv_sem)

        def take():
            here()
            total = slot_out[outer, :, first : first + width]
            if pairs <= UNROLL:
                for k in range(1, pairs):
                    total = total + slot_in[partner(outer, k, pairs), :, first : first + width]
            else:
                total = lax.fori_loop(
                    1,
                    pairs,
                    lambda k, so_far: so_far
                    + slot_in[partner(outer, k, pairs), :, first : first + width],
                    total,
                )
            data[:, own_x + first : own_x + first + width] = total

        return take

    def primal_step(step, tau, first, end):
        at = slice(first, end)
        gradient = gathered(
            (sel_h[at, : n_blk * wide_h], parts(vals_h[step])),
            (sel_t[at, : n_blk * wide_t], parts(vals_t[step])),
        )
        gradient = gradient + data[0, at]
        now = xw[at]
        new = jnp.minimum(jnp.maximum(now - tau * gradient, data[1, at]), data[2, at])
        xw[at] = new
        return (new - now) * (new - now)

    def dual_step(step, sigma):
        extrap = gathered((sel_y[:, : n_grp * wide_t], parts(vals_y[step])))
        now = ys[...]
        new = jnp.maximum(now + sigma * (rows_data[0] - extrap), rows_data[1])
        ys[...] = new
        return full_sum((new - now) * (new - now))

    weight = jnp.ones((1, 1), F32)
    waiter(raw.at[:nk], tile_sem.at[0])()
    y_here()
    transposed_here = transposed(0)
    repeat(1, pairs - 1, x_relay)
    planes_here()
    ids_x_here()
    picked()
    take_k = hand_out(0, wide_t)
    x_relay(pairs - 1)
    selectors()
    waiter(raw.at[nk:], tile_sem.at[1])()
    x_here()
    for ids, first in ((q_cols, first_q), (c_cols, first_k)):
        for p, tile_id in enumerate(ids):
            begin = first + p * quarters
            xw[begin : begin + quarters] = xs[pl.ds(tile_id * quarters, quarters)]
    hessian_here = hessian(0)
    take_q = hand_out(q_first, wide_h)

    def keep(at, piece):
        cons_now[at, :] = piece

    constraint_now(keep)
    take_k()
    for step in range(ITERS):
        hessian_here()
        transposed_here()
        if step > 0:
            dual_here()
            total = scalar_sum(sums_x, step - 1, n_blk)
            ratio = (total[:, :1] + EPSILON) / (total[:, LANES // 2 : LANES // 2 + 1] + EPSILON)
            weight = jnp.sqrt(weight * jnp.sqrt(ratio))
        tau = STEP_SCALE / weight
        moved = full_sum(primal_step(step, tau, 0, first_q)[:own_x])
        constraint_here = constraint(step)
        primal_here = spread("grp", sums_y, step, moved)
        if step < ITERS - 1:
            take_q()
            primal_step(step, tau, first_q, last)
            hessian_here = hessian(step + 1)
        else:
            x_done = pltpu.make_async_copy(xw.at[:own_x], x_out, io_sem.at[0])
            x_done.start()
        if step == 0:
            rows_here()
            leaving.pop(0)()
        constraint_here()
        gone = dual_step(step, STEP_SCALE * weight)
        primal_here()
        lane = lax.broadcasted_iota(jnp.int32, (1, LANES), 1)
        moved = jnp.where(lane < LANES // 2, gone, scalar_sum(sums_y, step, n_grp))
        dual_here = spread("blk", sums_x, step, moved)
        if step < ITERS - 1:
            transposed_here = transposed(step + 1)
    y_done = pltpu.make_async_copy(ys.at[part(grp, own_y)], y_out, io_sem.at[1])
    y_done.start()
    dual_here()
    total = scalar_sum(sums_x, ITERS - 1, n_blk)
    ratio = (total[:, :1] + EPSILON) / (total[:, LANES // 2 : LANES // 2 + 1] + EPSILON)
    weight_out[...] = jnp.sqrt(weight * jnp.sqrt(ratio))
    w_done = pltpu.make_async_copy(weight_out, w_out, io_sem.at[2])
    w_done.start()
    for leave in leaving:
        leave()
    for item in (x_done, y_done, w_done):
        item.wait()


def shards(
    primal,
    dual,
    objective,
    lower,
    upper,
    bound_kind,
    rhs,
    row_kind,
    q_tiles,
    q_index,
    k_tiles,
    k_rows,
    k_cols,
):
    n_blk, n_grp = lax.axis_size("blk"), lax.axis_size("grp")
    nq, nk, tile = q_tiles.shape[1], k_tiles.shape[1], q_tiles.shape[-1]
    quarters = tile // LANES
    own_x, own_y = primal.shape[0] // LANES, dual.shape[0] // LANES
    wide_h, wide_t = nq * quarters, nk * quarters
    code_h, code_t = up(n_blk * wide_h, LANES), up(n_blk * wide_t, LANES)
    code_y = up(n_grp * wide_t, LANES)
    slots = up(wide_t, 16) + wide_h
    pairs = n_blk // 2
    hbm = pl.BlockSpec(memory_space=pl.ANY)

    def lanes(values):
        return values.reshape(-1, LANES)

    x, y, weight = pl.pallas_call(
        functools.partial(kernel, n_blk, n_grp),
        out_shape=(
            jax.ShapeDtypeStruct((own_x, LANES), F32),
            jax.ShapeDtypeStruct((own_y, LANES), F32),
            jax.ShapeDtypeStruct((1, 1), F32),
        ),
        in_specs=[hbm] * 13,
        out_specs=(hbm, hbm, hbm),
        scratch_shapes=[
            pltpu.VMEM((nk + nq, tile, tile), F32),
            pltpu.VMEM((own_x, LANES), jnp.int32),
            pltpu.VMEM((own_y, LANES), jnp.int32),
            pltpu.VMEM((1, 1), F32),
            pltpu.SMEM((2, nq), jnp.int32),
            pltpu.SMEM((1, nk), jnp.int32),
            pltpu.SMEM((1, nk), jnp.int32),
            pltpu.VMEM((n_blk * own_x, LANES), F32),
            pltpu.VMEM((n_grp * own_y, LANES), F32),
            pltpu.VMEM((own_x + slots, LANES), F32),
            pltpu.VMEM((3, 2 * own_x, LANES), F32),
            pltpu.VMEM((3, own_x + slots, LANES), F32),
            pltpu.VMEM((2, n_grp * own_y, LANES), F32),
            pltpu.VMEM((pairs, 3, slots, LANES), F32),
            pltpu.VMEM((pairs, 3, slots, LANES), F32),
            pltpu.VMEM((n_blk, (code_h + code_t) // LANES + 1, LANES), jnp.int32),
            pltpu.VMEM((n_grp, code_y // LANES, LANES), jnp.int32),
            pltpu.VMEM((own_x + slots, code_h), BF16),
            pltpu.VMEM((own_x + slots, code_t), BF16),
            pltpu.VMEM((n_grp * own_y, code_y), BF16),
            pltpu.VMEM((ITERS, n_blk * wide_h, LANES), F32),
            pltpu.VMEM((ITERS, n_blk * wide_t, LANES), F32),
            pltpu.VMEM((ITERS, n_grp * wide_t, LANES), F32),
            pltpu.VMEM((ITERS, n_blk, 1, LANES), F32),
            pltpu.VMEM((ITERS, n_grp, 1, LANES), F32),
            pltpu.VMEM((wide_t, LANES), F32),
            pltpu.SemaphoreType.DMA((2,)),
            pltpu.SemaphoreType.DMA((11,)),
            pltpu.SemaphoreType.DMA((pairs,)),
            pltpu.SemaphoreType.DMA((5,)),
            pltpu.SemaphoreType.DMA((5,)),
            pltpu.SemaphoreType.DMA((3 * ITERS + 1,)),
            pltpu.SemaphoreType.DMA((3 * ITERS + 1,)),
            pltpu.SemaphoreType.DMA((2 * ITERS + 3,)),
            pltpu.SemaphoreType.DMA((2 * ITERS + 3,)),
        ],
        compiler_params=pltpu.CompilerParams(
            collective_id=0, has_side_effects=True, vmem_limit_bytes=60 * 1024 * 1024
        ),
    )(
        lanes(primal),
        lanes(dual),
        lanes(objective),
        lanes(lower),
        lanes(upper),
        lanes(bound_kind),
        lanes(rhs),
        lanes(row_kind),
        q_index[0],
        k_rows,
        k_cols,
        q_tiles[0],
        k_tiles[0],
    )
    return x.reshape(-1), y.reshape(-1), weight.reshape(())


def solution(mesh):
    vector = P(("blk", "grp"))
    return jax.shard_map(
        shards,
        mesh=mesh,
        in_specs=(vector,) * 8
        + (
            P("grp", "blk", None, None),
            P("grp", None, "blk"),
            P("grp", "blk", None, None),
            P("grp", "blk"),
            P("grp", "blk"),
        ),
        out_specs=(vector, vector, P()),
        check_vma=False,
    )
```

time: 51.3 us -> 42 us (0.82)
  Pallas kernels: 45.8 us -> 36.6 us
    pallas_call x1, Pallas kernels: 45.8 us -> 36.6 us  [shards(): pl.pallas_call(functools.partial(kernel, n_blk, n_grp), out_shape=(jax.Sh...]
where the time goes in v2:
time: 42 us; the launch traced here: 41.7 us
  Pallas kernels  36.6 us (87%)
  local copies, waits for them, and re-layouts  2.7 us (6%)
  between operations  2.38 us (6%)
    pallas_call x1, Pallas kernels, shards(): pl.pallas_call(functools.partial(kernel, n_blk, n_grp), out_shape=(jax.Sh...  36.6 us
    unnamed x2, local copies, waits for them, and re-layouts  2.7 us

profile of v2, /device:TPU:0, one launch (start us, length us, event | category | flops | bytes accessed | tf_op | source)
XLA Modules:
  0.0 41.7 jit_solution(425634920389892523)
XLA Ops:
  0.6 36.6 %shard_map.148 = (f32[64,128]{1,0:T(8,128)}, f32[32,128]{1,0:T(8,128)}, f32[1,1]{1,0:T(1,128)}) custom-call(f32[64,128]{1,0:T(8,128)} %bitcast.16, f32[32,128]{1,0:T(8,128)} %bitcast.22, f32[64,128]{1,0:T(8,128)} %bitcast.17, f32[64,128]{1,0:T(8,128)} %bitcast.18, f32[64,128]{1,0:T(8,128)} %bitcast.19, s32[64,128]{1,0:T(8,128)} %bitcast.20, ...), custom_call_target="tpu_custom_call" | custom-call | tf_op jit(solution)/shard_map/pallas_call | solution.py:560
  37.2 1.4 %copy.19 = f32[8192]{0:T(1024)} copy(f32[8192]{0:T(1024)} %bitcast.21) | data formatting | bytes 65536
  38.6 1.3 %copy.20 = f32[4096]{0:T(1024)} copy(f32[4096]{0:T(1024)} %bitcast.25) | data formatting | bytes 32768

commit v3 on v2

--- a/solution.py
+++ b/solution.py
@@ -87,7 +87,6 @@
     raw,
     kinds,
     row_kinds,
-    weight_out,
     q_at,
     r_at,
     c_at,
@@ -124,6 +123,7 @@
     nq, nk = q_tiles.shape[0], k_tiles.shape[0]
     quarters = q_tiles.shape[-1] // LANES
     own_x, own_y = primal.shape[0], dual.shape[0]
+    half_x = own_x // 2
     wide_h, wide_t = nq * quarters, nk * quarters
     pairs = n_blk // 2
     outer, inner = lax.div(blk, 2), lax.rem(blk, 2)
@@ -157,7 +157,8 @@
     for at, (source, target) in enumerate(
         (
             (dual, ys.at[part(grp, own_y)]),
-            (primal, xs.at[part(blk, own_x)]),
+            (primal.at[:half_x], xs.at[0, blk]),
+            (primal.at[half_x:], xs.at[1, blk]),
             (q_index, q_at),
             (k_rows, r_at),
             (k_cols, c_at),
@@ -214,20 +215,28 @@
             device_id_type=MESH,
         ).start()
 
-    def share(axis, mine, others):
+    def channel(axis, others):
         at = used[axis]
         used[axis] += 1
         count, me = (n_blk, blk) if axis == "blk" else (n_grp, grp)
         sends, recvs = (blk_send, blk_recv) if axis == "blk" else (grp_send, grp_recv)
-        repeat(
-            1,
-            count,
-            lambda k: send(
-                axis, partner(me, count - k, count), mine, mine, sends.at[at], recvs.at[at]
-            ),
-        )
         leaving.append(waiter(others, sends.at[at]))
-        return waiter(others, recvs.at[at])
+
+        def post(mine):
+            repeat(
+                1,
+                count,
+                lambda k: send(
+                    axis, partner(me, count - k, count), mine, mine, sends.at[at], recvs.at[at]
+                ),
+            )
+
+        return post, waiter(others, recvs.at[at])
+
+    def share(axis, mine, others):
+        post, here = channel(axis, others)
+        post(mine)
+        return here
 
     def single():
         used["one"] += 1
@@ -236,33 +245,34 @@
     y_here = share("grp", ys.at[part(grp, own_y)], ys.at[: (n_grp - 1) * own_y])
     ids_x_here = share("blk", ids_x.at[blk], ids_x.at[: n_blk - 1])
 
-    far_send = single()[0]
-    near_send, near_recv = single()
-
-    def x_slot(s):
-        return xs.at[part(s, own_x)]
-
-    def x_far(k):
-        send(
-            "blk",
-            partner(outer, pairs - k, pairs) * 2 + inner,
-            x_slot(blk),
-            x_slot(blk),
-            far_send,
-            far_recv.at[outer],
-        )
-
-    def x_relay(k):
-        there = partner(outer, k, pairs)
-        source = x_slot(there * 2 + inner)
-        waiter(source, far_recv.at[there])()
-        send("blk", beside, source, source, near_send, near_recv)
-
-    repeat(1, pairs, x_far)
-    send("blk", beside, x_slot(blk), x_slot(blk), near_send, near_recv)
-    x_here = waiter(xs.at[: pairs * own_x], near_recv)
-    leaving.append(waiter(xs.at[: (pairs - 1) * own_x], far_send))
-    leaving.append(waiter(xs.at[: pairs * own_x], near_send))
+    def column(ref, recvs):
+        far_send = single()[0]
+        near_send, near_recv = single()
+        leaving.append(waiter(ref.at[: pairs - 1], far_send))
+        leaving.append(waiter(ref.at[:pairs], near_send))
+
+        def far():
+            def one(k):
+                there = partner(outer, pairs - k, pairs) * 2 + inner
+                send("blk", there, ref.at[blk], ref.at[blk], far_send, recvs.at[outer])
+
+            repeat(1, pairs, one)
+
+        def near():
+            send("blk", beside, ref.at[blk], ref.at[blk], near_send, near_recv)
+
+        def relay(k):
+            there = partner(outer, k, pairs)
+            source = ref.at[there * 2 + inner]
+            waiter(source, recvs.at[there])()
+            send("blk", beside, source, source, near_send, near_recv)
+
+        return far, near, relay, waiter(ref.at[:pairs], near_recv)
+
+    lots = [column(xs.at[half], far_recv.at[half]) for half in range(xs.shape[0])]
+    for x_far, x_near, _, _ in lots:
+        x_far()
+        x_near()
 
     planes_send, planes_recv = single()
     planes = both.at[:, mine_pair]
@@ -275,7 +285,8 @@
         "grp", rows_data.at[:, part(grp, own_y)], rows_data.at[:, : (n_grp - 1) * own_y]
     )
 
-    xw[:own_x] = xs[part(blk, own_x)]
+    xw[:half_x] = xs[0, blk]
+    xw[half_x:own_x] = xs[1, blk]
     data[:, :own_x] = both[:, mine_pair]
     xw[first_k + wide_t : first_q] = jnp.zeros((q_first - wide_t, LANES), F32)
     data[:, first_k + wide_t : first_q] = jnp.zeros((3, q_first - wide_t, LANES), F32)
@@ -306,38 +317,44 @@
                 total.append(folded(piece.T))
         return [jnp.sum(piece, axis=0, keepdims=True) for piece in total]
 
-    def row_block(ref, step, index, size):
-        return ref.at[step, pl.ds(pl.multiple_of(index * size, 8), size)]
+    def computed(count, mine, post, one):
+        for p in range(count):
+            one(p)
+        post(mine)
+
+    def transpose_one(step, p):
+        for q, piece in enumerate(product(ys, c_rows[p] * quarters, p, True)):
+            vals_t[step, blk, pl.ds(p * quarters + q, 1), :] = -piece
 
     def transposed(step):
-        mine = row_block(vals_t, step, blk, wide_t)
-        for p in range(nk):
-            for q, piece in enumerate(product(ys, c_rows[p] * quarters, p, True)):
-                mine[pl.ds(p * quarters + q, 1), :] = -piece
-        return share("blk", mine, vals_t.at[step, : (n_blk - 1) * wide_t])
+        post, here = channel("blk", vals_t.at[step, : n_blk - 1])
+        computed(nk, vals_t.at[step, blk], post, lambda p: transpose_one(step, p))
+        return here
 
     def hessian(step):
-        mine = row_block(vals_h, step, blk, wide_h)
-        for p in range(nq):
+        post, here = channel("blk", vals_h.at[step, : n_blk - 1])
+
+        def one(p):
             for q, piece in enumerate(product(xw, first_q + p * quarters, nk + p, False)):
-                mine[pl.ds(p * quarters + q, 1), :] = piece
-        return share("blk", mine, vals_h.at[step, : (n_blk - 1) * wide_h])
-
-    def constraint_now(call):
-        for p in range(nk):
-            for q, piece in enumerate(product(xw, first_k + p * quarters, p, False)):
-                call(pl.ds(p * quarters + q, 1), piece)
+                vals_h[step, blk, pl.ds(p * quarters + q, 1), :] = piece
+
+        computed(nq, vals_h.at[step, blk], post, one)
+        return here
+
+    def constraint_one(p, call):
+        for q, piece in enumerate(product(xw, first_k + p * quarters, p, False)):
+            call(pl.ds(p * quarters + q, 1), piece)
 
     def constraint(step):
-        mine = row_block(vals_y, step, grp, wide_t)
+        post, here = channel("grp", vals_y.at[step, : n_grp - 1])
 
         def put(at, piece):
-            mine[at, :] = 2.0 * piece - cons_now[at, :]
+            vals_y[step, grp, at, :] = 2.0 * piece - cons_now[at, :]
             if step < ITERS - 1:
                 cons_now[at, :] = piece
 
-        constraint_now(put)
-        return share("grp", mine, vals_y.at[step, : (n_grp - 1) * wide_t])
+        computed(nk, vals_y.at[step, grp], post, lambda p: constraint_one(p, put))
+        return here
 
     def spread(axis, ref, step, value):
         me, count = (blk, n_blk) if axis == "blk" else (grp, n_grp)
@@ -443,8 +460,8 @@
     def primal_step(step, tau, first, end):
         at = slice(first, end)
         gradient = gathered(
-            (sel_h[at, : n_blk * wide_h], parts(vals_h[step])),
-            (sel_t[at, : n_blk * wide_t], parts(vals_t[step])),
+            (sel_h[at, : n_blk * wide_h], parts(vals_h[step].reshape(n_blk * wide_h, LANES))),
+            (sel_t[at, : n_blk * wide_t], parts(vals_t[step].reshape(n_blk * wide_t, LANES))),
         )
         gradient = gradient + data[0, at]
         now = xw[at]
@@ -453,36 +470,47 @@
         return (new - now) * (new - now)
 
     def dual_step(step, sigma):
-        extrap = gathered((sel_y[:, : n_grp * wide_t], parts(vals_y[step])))
+        extrap = gathered((sel_y[:, : n_grp * wide_t], parts(vals_y[step].reshape(n_grp * wide_t, LANES))))
         now = ys[...]
         new = jnp.maximum(now + sigma * (rows_data[0] - extrap), rows_data[1])
         ys[...] = new
         return full_sum((new - now) * (new - now))
 
     weight = jnp.ones((1, 1), F32)
+    repeat(1, pairs, lots[0][2])
     waiter(raw.at[:nk], tile_sem.at[0])()
     y_here()
-    transposed_here = transposed(0)
-    repeat(1, pairs - 1, x_relay)
+    for p in range(nk):
+        transpose_one(0, p)
+    t_far, t_near, t_relay, transposed_here = column(vals_t.at[0], far_recv.at[2])
+    t_far()
+    repeat(1, pairs, lots[1][2])
+    t_near()
     planes_here()
     ids_x_here()
     picked()
     take_k = hand_out(0, wide_t)
-    x_relay(pairs - 1)
     selectors()
     waiter(raw.at[nk:], tile_sem.at[1])()
-    x_here()
+    lots[0][3]()
+    lots[1][3]()
     for ids, first in ((q_cols, first_q), (c_cols, first_k)):
         for p, tile_id in enumerate(ids):
             begin = first + p * quarters
-            xw[begin : begin + quarters] = xs[pl.ds(tile_id * quarters, quarters)]
+            piece = lax.div(tile_id * quarters, half_x)
+            at = lax.rem(tile_id * quarters, half_x)
+            xw[begin : begin + quarters] = xs[
+                lax.rem(piece, 2), lax.div(piece, 2), pl.ds(at, quarters)
+            ]
     hessian_here = hessian(0)
     take_q = hand_out(q_first, wide_h)
+    repeat(1, pairs, t_relay)
 
     def keep(at, piece):
         cons_now[at, :] = piece
 
-    constraint_now(keep)
+    for p in range(nk):
+        constraint_one(p, keep)
     take_k()
     for step in range(ITERS):
         hessian_here()
@@ -501,8 +529,7 @@
             primal_step(step, tau, first_q, last)
             hessian_here = hessian(step + 1)
         else:
-            x_done = pltpu.make_async_copy(xw.at[:own_x], x_out, io_sem.at[0])
-            x_done.start()
+            x_out[...] = xw[:own_x]
         if step == 0:
             rows_here()
             leaving.pop(0)()
@@ -514,18 +541,25 @@
         dual_here = spread("blk", sums_x, step, moved)
         if step < ITERS - 1:
             transposed_here = transposed(step + 1)
-    y_done = pltpu.make_async_copy(ys.at[part(grp, own_y)], y_out, io_sem.at[1])
-    y_done.start()
+    y_out[...] = ys[part(grp, own_y)]
     dual_here()
     total = scalar_sum(sums_x, ITERS - 1, n_blk)
     ratio = (total[:, :1] + EPSILON) / (total[:, LANES // 2 : LANES // 2 + 1] + EPSILON)
-    weight_out[...] = jnp.sqrt(weight * jnp.sqrt(ratio))
-    w_done = pltpu.make_async_copy(weight_out, w_out, io_sem.at[2])
-    w_done.start()
+    w_out[...] = jnp.broadcast_to(jnp.sqrt(weight * jnp.sqrt(ratio)), w_out.shape)
     for leave in leaving:
         leave()
-    for item in (x_done, y_done, w_done):
-        item.wait()
+
+
+def settle(x, y, weight, x_out, y_out, w_out, single, sems):
+    single[...] = weight[:1, :1]
+    copies = [
+        pltpu.make_async_copy(source, target, sems.at[at])
+        for at, (source, target) in enumerate(((x, x_out), (y, y_out), (single, w_out)))
+    ]
+    for copy in copies:
+        copy.start()
+    for copy in copies:
+        copy.wait()
 
 
 def shards(
@@ -552,7 +586,8 @@
     code_y = up(n_grp * wide_t, LANES)
     slots = up(wide_t, 16) + wide_h
     pairs = n_blk // 2
-    hbm = pl.BlockSpec(memory_space=pl.ANY)
+    hbm = pl.BlockSpec(memory_space=pltpu.HBM)
+    vmem = pl.BlockSpec(memory_space=pltpu.VMEM)
 
     def lanes(values):
         return values.reshape(-1, LANES)
@@ -562,19 +597,18 @@
         out_shape=(
             jax.ShapeDtypeStruct((own_x, LANES), F32),
             jax.ShapeDtypeStruct((own_y, LANES), F32),
-            jax.ShapeDtypeStruct((1, 1), F32),
+            jax.ShapeDtypeStruct((8, LANES), F32),
         ),
         in_specs=[hbm] * 13,
-        out_specs=(hbm, hbm, hbm),
+        out_specs=(vmem, vmem, vmem),
         scratch_shapes=[
             pltpu.VMEM((nk + nq, tile, tile), F32),
             pltpu.VMEM((own_x, LANES), jnp.int32),
             pltpu.VMEM((own_y, LANES), jnp.int32),
-            pltpu.VMEM((1, 1), F32),
             pltpu.SMEM((2, nq), jnp.int32),
             pltpu.SMEM((1, nk), jnp.int32),
             pltpu.SMEM((1, nk), jnp.int32),
-            pltpu.VMEM((n_blk * own_x, LANES), F32),
+            pltpu.VMEM((2, n_blk, own_x // 2, LANES), F32),
             pltpu.VMEM((n_grp * own_y, LANES), F32),
             pltpu.VMEM((own_x + slots, LANES), F32),
             pltpu.VMEM((3, 2 * own_x, LANES), F32),
@@ -587,40 +621,52 @@
             pltpu.VMEM((own_x + slots, code_h), BF16),
             pltpu.VMEM((own_x + slots, code_t), BF16),
             pltpu.VMEM((n_grp * own_y, code_y), BF16),
-            pltpu.VMEM((ITERS, n_blk * wide_h, LANES), F32),
-            pltpu.VMEM((ITERS, n_blk * wide_t, LANES), F32),
-            pltpu.VMEM((ITERS, n_grp * wide_t, LANES), F32),
+            pltpu.VMEM((ITERS, n_blk, wide_h, LANES), F32),
+            pltpu.VMEM((ITERS, n_blk, wide_t, LANES), F32),
+            pltpu.VMEM((ITERS, n_grp, wide_t, LANES), F32),
             pltpu.VMEM((ITERS, n_blk, 1, LANES), F32),
             pltpu.VMEM((ITERS, n_grp, 1, LANES), F32),
             pltpu.VMEM((wide_t, LANES), F32),
             pltpu.SemaphoreType.DMA((2,)),
-            pltpu.SemaphoreType.DMA((11,)),
-            pltpu.SemaphoreType.DMA((pairs,)),
-            pltpu.SemaphoreType.DMA((5,)),
-            pltpu.SemaphoreType.DMA((5,)),
-            pltpu.SemaphoreType.DMA((3 * ITERS + 1,)),
-            pltpu.SemaphoreType.DMA((3 * ITERS + 1,)),
+            pltpu.SemaphoreType.DMA((12,)),
+            pltpu.SemaphoreType.DMA((3, pairs)),
+            pltpu.SemaphoreType.DMA((9,)),
+            pltpu.SemaphoreType.DMA((9,)),
+            pltpu.SemaphoreType.DMA((3 * ITERS,)),
+            pltpu.SemaphoreType.DMA((3 * ITERS,)),
             pltpu.SemaphoreType.DMA((2 * ITERS + 3,)),
             pltpu.SemaphoreType.DMA((2 * ITERS + 3,)),
         ],
         compiler_params=pltpu.CompilerParams(
-            collective_id=0, has_side_effects=True, vmem_limit_bytes=60 * 1024 * 1024
+            collective_id=0, has_side_effects=True, vmem_limit_bytes=24 * 1024 * 1024
         ),
     )(
-        lanes(primal),
-        lanes(dual),
-        lanes(objective),
-        lanes(lower),
-        lanes(upper),
-        lanes(bound_kind),
-        lanes(rhs),
-        lanes(row_kind),
-        q_index[0],
-        k_rows,
-        k_cols,
-        q_tiles[0],
-        k_tiles[0],
+        *(
+            pltpu.with_memory_space_constraint(item, pltpu.HBM)
+            for item in (
+                lanes(primal),
+                lanes(dual),
+                lanes(objective),
+                lanes(lower),
+                lanes(upper),
+                lanes(bound_kind),
+                lanes(rhs),
+                lanes(row_kind),
+                q_index[0],
+                k_rows,
+                k_cols,
+                q_tiles[0],
+                k_tiles[0],
+            )
+        )
     )
+    x, y, weight = pl.pallas_call(
+        settle,
+        out_shape=tuple(jax.ShapeDtypeStruct(shape, F32) for shape in (x.shape, y.shape, (1, 1))),
+        in_specs=[vmem] * 3,
+        out_specs=(hbm,) * 3,
+        scratch_shapes=[pltpu.VMEM((1, 1), F32), pltpu.SemaphoreType.DMA((3,))],
+    )(*(pltpu.with_memory_space_constraint(item, pltpu.VMEM) for item in (x, y, weight)))
     return x.reshape(-1), y.reshape(-1), weight.reshape(())
 
 

time: 42 us -> 37.3 us (0.89)
  local copies, waits for them, and re-layouts: 2.7 us -> 0 us
  between operations: 2.38 us -> 0.64 us
    unnamed x2 -> x0, local copies, waits for them, and re-layouts: 2.7 us -> none
    pallas_call x1, Pallas kernels: 36.6 us -> 35.8 us  [shards(): pl.pallas_call(functools.partial(kernel, n_blk, n_grp), out_shape=(jax.Sh...]
    pallas_call x0 -> x1, Pallas kernels: none -> 0.65 us  [shards(): pl.pallas_call(settle, out_shape=tuple((jax.ShapeDtypeStruct(shape, F32)...]
where the time goes in v3:
time: 37.3 us; the launch traced here: 37.1 us
  Pallas kernels  36.4 us (98%)
  between operations  0.64 us (2%)
    pallas_call x1, Pallas kernels, shards(): pl.pallas_call(functools.partial(kernel, n_blk, n_grp), out_shape=(jax.Sh...  35.8 us

profile of v3, /device:TPU:0, one launch (start us, length us, event | category | flops | bytes accessed | tf_op | source)
XLA Modules:
  0.0 37.1 jit_solution(11969168166765337654)
XLA Ops:
  0.6 35.8 %shard_map.148 = (f32[64,128]{1,0:T(8,128)S(1)}, f32[32,128]{1,0:T(8,128)S(1)}, f32[8,128]{1,0:T(8,128)S(1)}) custom-call(f32[64,128]{1,0:T(8,128)} %bitcast.16, f32[32,128]{1,0:T(8,128)} %bitcast.21, f32[64,128]{1,0:T(8,128)} %bitcast.17, f32[64,128]{1,0:T(8,128)} %bitcast.18, f32[64,128]{1,0:T(8,128)} %bitcast.19, s32[64,128]{1,0:T(8,128)} %bitcast.20, ...), custom_call_target="tpu_custom_call" | custom-call | tf_op jit(solution)/shard_map/pallas_call | solution.py:595
  36.4 0.6 %shard_map.149 = (f32[64,128]{1,0:T(8,128)}, f32[32,128]{1,0:T(8,128)}, f32[1,1]{1,0:T(1,128)}) custom-call(f32[64,128]{1,0:T(8,128)S(1)} %get-tuple-element.9.x, f32[32,128]{1,0:T(8,128)S(1)} %get-tuple-element.10.y, f32[8,128]{1,0:T(8,128)S(1)} %get-tuple-element.11.weight), custom_call_target="tpu_custom_call" | custom-call | tf_op jit(solution)/shard_map/pallas_call | solution.py:663

commit v4 on v3

--- a/solution.py
+++ b/solution.py
@@ -1,4 +1,5 @@
 import functools
+import math
 
 import jax
 import jax.numpy as jnp
@@ -112,12 +113,12 @@
     tile_sem,
     io_sem,
     far_recv,
-    one_send,
     one_recv,
-    blk_send,
     blk_recv,
-    grp_send,
     grp_recv,
+    y_send,
+    all_send,
+    spare,
 ):
     blk, grp = lax.axis_index("blk"), lax.axis_index("grp")
     nq, nk = q_tiles.shape[0], k_tiles.shape[0]
@@ -183,14 +184,9 @@
     q_cols = [q_at[1, p] for p in range(nq)]
     c_rows = [r_at[0, p] for p in range(nk)]
     c_cols = [c_at[0, p] for p in range(nk)]
-    ids_x[blk, :code_h] = segment(q_rows, blk * wide_h, wide_h, code_h, quarters)
-    ids_x[blk, code_h : code_h + code_t] = segment(
-        c_cols, blk * wide_t, wide_t, code_t, quarters
-    )
-    wanted = c_cols + [-1] * ((q_first - wide_t) // quarters) + q_cols
-    ids_x[blk, code_h + code_t :] = segment(
-        wanted, 0, q_first + wide_h, ids_x.shape[1] - code_h - code_t, quarters
-    )
+    gap = [-1] * ((q_first - wide_t) // quarters)
+    listed = c_cols + gap + q_cols + q_rows
+    ids_x[blk] = segment(listed, 0, len(listed) * quarters, 1, quarters)
     ids_y[grp] = segment(c_rows, grp * wide_t, wide_t, ids_y.shape[1], quarters)
     kind = kinds[...]
     both[1, mine_pair] = jnp.where((kind == 1) | (kind == 2), both[1, mine_pair], -FREE)
@@ -199,7 +195,7 @@
 
     pl.semaphore_wait(barrier, n_blk + n_grp - 2)
 
-    leaving = []
+    sent = []
     used = {"blk": 0, "grp": 0, "one": 0}
 
     def waiter(ref, sem):
@@ -215,70 +211,74 @@
             device_id_type=MESH,
         ).start()
 
-    def channel(axis, others):
+    def leaves(ref, times):
+        sent.append(math.prod(ref.shape[:-1]) * times)
+
+    def channel(axis, others, leave=all_send):
         at = used[axis]
         used[axis] += 1
         count, me = (n_blk, blk) if axis == "blk" else (n_grp, grp)
-        sends, recvs = (blk_send, blk_recv) if axis == "blk" else (grp_send, grp_recv)
-        leaving.append(waiter(others, sends.at[at]))
+        recvs = blk_recv if axis == "blk" else grp_recv
+        if leave is all_send:
+            leaves(others, 1)
 
         def post(mine):
             repeat(
                 1,
                 count,
                 lambda k: send(
-                    axis, partner(me, count - k, count), mine, mine, sends.at[at], recvs.at[at]
+                    axis, partner(me, count - k, count), mine, mine, leave.at[0], recvs.at[at]
                 ),
             )
 
         return post, waiter(others, recvs.at[at])
 
-    def share(axis, mine, others):
-        post, here = channel(axis, others)
+    def share(axis, mine, others, leave=all_send):
+        post, here = channel(axis, others, leave)
         post(mine)
         return here
 
     def single():
         used["one"] += 1
-        return one_send.at[used["one"] - 1], one_recv.at[used["one"] - 1]
-
-    y_here = share("grp", ys.at[part(grp, own_y)], ys.at[: (n_grp - 1) * own_y])
+        return one_recv.at[used["one"] - 1]
+
+    y_rest = ys.at[: (n_grp - 1) * own_y]
+    y_here = share("grp", ys.at[part(grp, own_y)], y_rest, y_send)
     ids_x_here = share("blk", ids_x.at[blk], ids_x.at[: n_blk - 1])
 
     def column(ref, recvs):
-        far_send = single()[0]
-        near_send, near_recv = single()
-        leaving.append(waiter(ref.at[: pairs - 1], far_send))
-        leaving.append(waiter(ref.at[:pairs], near_send))
+        near_recv = single()
+        leaves(ref.at[0], 2 * pairs - 1)
 
         def far():
             def one(k):
                 there = partner(outer, pairs - k, pairs) * 2 + inner
-                send("blk", there, ref.at[blk], ref.at[blk], far_send, recvs.at[outer])
+                send("blk", there, ref.at[blk], ref.at[blk], all_send.at[0], recvs.at[outer])
 
             repeat(1, pairs, one)
 
         def near():
-            send("blk", beside, ref.at[blk], ref.at[blk], near_send, near_recv)
+            send("blk", beside, ref.at[blk], ref.at[blk], all_send.at[0], near_recv)
 
         def relay(k):
             there = partner(outer, k, pairs)
             source = ref.at[there * 2 + inner]
             waiter(source, recvs.at[there])()
-            send("blk", beside, source, source, near_send, near_recv)
+            send("blk", beside, source, source, all_send.at[0], near_recv)
 
         return far, near, relay, waiter(ref.at[:pairs], near_recv)
 
     lots = [column(xs.at[half], far_recv.at[half]) for half in range(xs.shape[0])]
-    for x_far, x_near, _, _ in lots:
+    for x_far, _, _, _ in lots:
         x_far()
+
+    planes_recv = single()
+    planes = both.at[:, mine_pair]
+    send("blk", beside, planes, planes, all_send.at[0], planes_recv)
+    planes_here = waiter(planes, planes_recv)
+    leaves(planes, 1)
+    for _, x_near, _, _ in lots:
         x_near()
-
-    planes_send, planes_recv = single()
-    planes = both.at[:, mine_pair]
-    send("blk", beside, planes, planes, planes_send, planes_recv)
-    planes_here = waiter(planes, planes_recv)
-    leaving.append(waiter(planes, planes_send))
 
     ids_y_here = share("grp", ids_y.at[grp], ids_y.at[: n_grp - 1])
     rows_here = share(
@@ -385,9 +385,18 @@
                 place == codes[k : k + 1, :], 1.0, 0.0
             ).astype(BF16)
 
+    def lined_up(first, width, rows):
+        place = lax.broadcasted_iota(jnp.int32, (rows, LANES), 0) * LANES
+        place = place + lax.broadcasted_iota(jnp.int32, (rows, LANES), 1)
+        result = jnp.zeros((rows, LANES), jnp.int32)
+        for s in range(n_blk):
+            moved = pltpu.roll(ids_x[s], (s * width - first) % LANES, 1)
+            inside = (place >= s * width) & (place < (s + 1) * width)
+            result = jnp.where(inside, jnp.broadcast_to(moved, (rows, LANES)), result)
+        return result
+
     def selectors():
         ids_y_here()
-        codes = jnp.sum(ids_x[:, : code_h + code_t], axis=0)
         line = lax.broadcasted_iota(jnp.int32, (last, LANES), 0)
         place = jnp.where(line < own_x, line + blk * own_x, -1)
         for ids, first in ((c_cols, first_k), (q_cols, first_q)):
@@ -395,8 +404,8 @@
                 begin = first + p * quarters
                 inside = (line >= begin) & (line < begin + quarters)
                 place = jnp.where(inside, line - begin + tile_id * quarters, place)
-        selector(sel_h, place, codes[:code_h])
-        selector(sel_t, place, codes[code_h:])
+        selector(sel_h, place, lined_up(q_first + wide_h, wide_h, code_h))
+        selector(sel_t, place, lined_up(0, wide_t, code_t))
         line = lax.broadcasted_iota(jnp.int32, (sel_y.shape[0], LANES), 0)
         selector(sel_y, line, jnp.sum(ids_y[...], axis=0))
 
@@ -408,7 +417,7 @@
 
         def one(k):
             there = partner(outer, k, pairs)
-            codes = ids_x[there * 2 + inner, code_h + code_t :]
+            codes = ids_x[there * 2 + inner]
             hits = jnp.where(line == codes, 1.0, 0.0).T[: slot_out.shape[2]].astype(BF16)
             taken = jnp.dot(hits, values, preferred_element_type=F32)
             for plane in range(3):
@@ -421,7 +430,7 @@
         repeat(0, pairs, one)
 
     def hand_out(first, width):
-        send_sem, recv_sem = single()
+        recv_sem = single()
 
         def one(k):
             there = partner(outer, pairs - k, pairs)
@@ -430,13 +439,13 @@
                 there * 2 + inner,
                 slot_out.at[there, :, first : first + width],
                 slot_in.at[outer, :, first : first + width],
-                send_sem,
+                all_send.at[0],
                 recv_sem,
             )
 
         repeat(1, pairs, one)
         whole = slot_in.at[: pairs - 1, :, first : first + width]
-        leaving.append(waiter(whole, send_sem))
+        leaves(whole, 1)
         here = waiter(whole, recv_sem)
 
         def take():
@@ -503,7 +512,6 @@
                 lax.rem(piece, 2), lax.div(piece, 2), pl.ds(at, quarters)
             ]
     hessian_here = hessian(0)
-    take_q = hand_out(q_first, wide_h)
     repeat(1, pairs, t_relay)
 
     def keep(at, piece):
@@ -511,6 +519,7 @@
 
     for p in range(nk):
         constraint_one(p, keep)
+    take_q = hand_out(q_first, wide_h)
     take_k()
     for step in range(ITERS):
         hessian_here()
@@ -532,7 +541,7 @@
             x_out[...] = xw[:own_x]
         if step == 0:
             rows_here()
-            leaving.pop(0)()
+            waiter(y_rest, y_send.at[0])()
         constraint_here()
         gone = dual_step(step, STEP_SCALE * weight)
         primal_here()
@@ -546,8 +555,7 @@
     total = scalar_sum(sums_x, ITERS - 1, n_blk)
     ratio = (total[:, :1] + EPSILON) / (total[:, LANES // 2 : LANES // 2 + 1] + EPSILON)
     w_out[...] = jnp.broadcast_to(jnp.sqrt(weight * jnp.sqrt(ratio)), w_out.shape)
-    for leave in leaving:
-        leave()
+    waiter(spare.at[: sum(sent)], all_send.at[0])()
 
 
 def settle(x, y, weight, x_out, y_out, w_out, single, sems):
@@ -586,6 +594,10 @@
     code_y = up(n_grp * wide_t, LANES)
     slots = up(wide_t, 16) + wide_h
     pairs = n_blk // 2
+    sent = (n_blk - 1) * (1 + (ITERS - 1) * wide_t + ITERS * (wide_h + 1))
+    sent += (n_grp - 1) * (code_y // LANES + 2 * own_y + ITERS * (wide_t + 1))
+    sent += (2 * pairs - 1) * (own_x + wide_t) + 3 * own_x
+    sent += (pairs - 1) * 3 * (wide_t + wide_h)
     hbm = pl.BlockSpec(memory_space=pltpu.HBM)
     vmem = pl.BlockSpec(memory_space=pltpu.VMEM)
 
@@ -616,7 +628,7 @@
             pltpu.VMEM((2, n_grp * own_y, LANES), F32),
             pltpu.VMEM((pairs, 3, slots, LANES), F32),
             pltpu.VMEM((pairs, 3, slots, LANES), F32),
-            pltpu.VMEM((n_blk, (code_h + code_t) // LANES + 1, LANES), jnp.int32),
+            pltpu.VMEM((n_blk, 1, LANES), jnp.int32),
             pltpu.VMEM((n_grp, code_y // LANES, LANES), jnp.int32),
             pltpu.VMEM((own_x + slots, code_h), BF16),
             pltpu.VMEM((own_x + slots, code_t), BF16),
@@ -630,15 +642,15 @@
             pltpu.SemaphoreType.DMA((2,)),
             pltpu.SemaphoreType.DMA((12,)),
             pltpu.SemaphoreType.DMA((3, pairs)),
-            pltpu.SemaphoreType.DMA((9,)),
-            pltpu.SemaphoreType.DMA((9,)),
-            pltpu.SemaphoreType.DMA((3 * ITERS,)),
+            pltpu.SemaphoreType.DMA((6,)),
             pltpu.SemaphoreType.DMA((3 * ITERS,)),
             pltpu.SemaphoreType.DMA((2 * ITERS + 3,)),
-            pltpu.SemaphoreType.DMA((2 * ITERS + 3,)),
+            pltpu.SemaphoreType.DMA((1,)),
+            pltpu.SemaphoreType.DMA((1,)),
+            pltpu.VMEM((sent, LANES), F32),
         ],
         compiler_params=pltpu.CompilerParams(
-            collective_id=0, has_side_effects=True, vmem_limit_bytes=24 * 1024 * 1024
+            collective_id=0, has_side_effects=True, vmem_limit_bytes=40 * 1024 * 1024
         ),
     )(
         *(

time: 37.3 us -> 36.8 us (0.987)
  Pallas kernels: 36.4 us -> 35.9 us
    pallas_call x1, Pallas kernels: 35.8 us -> 35.3 us  [shards(): pl.pallas_call(functools.partial(kernel, n_blk, n_grp), out_shape=(jax.Sh...]
where the time goes in v4:
time: 36.8 us; the launch traced here: 36.6 us
  Pallas kernels  35.9 us (98%)
  between operations  0.64 us (2%)
    pallas_call x1, Pallas kernels, shards(): pl.pallas_call(functools.partial(kernel, n_blk, n_grp), out_shape=(jax.Sh...  35.3 us

profile of v4, /device:TPU:0, one launch (start us, length us, event | category | flops | bytes accessed | tf_op | source)
XLA Modules:
  0.0 36.6 jit_solution(2535029841030959855)
XLA Ops:
  0.6 35.3 %shard_map.148 = (f32[64,128]{1,0:T(8,128)S(1)}, f32[32,128]{1,0:T(8,128)S(1)}, f32[8,128]{1,0:T(8,128)S(1)}) custom-call(f32[64,128]{1,0:T(8,128)} %bitcast.16, f32[32,128]{1,0:T(8,128)} %bitcast.21, f32[64,128]{1,0:T(8,128)} %bitcast.17, f32[64,128]{1,0:T(8,128)} %bitcast.18, f32[64,128]{1,0:T(8,128)} %bitcast.19, s32[64,128]{1,0:T(8,128)} %bitcast.20, ...), custom_call_target="tpu_custom_call" | custom-call | tf_op jit(solution)/shard_map/pallas_call | solution.py:607
  35.9 0.6 %shard_map.149 = (f32[64,128]{1,0:T(8,128)}, f32[32,128]{1,0:T(8,128)}, f32[1,1]{1,0:T(1,128)}) custom-call(f32[64,128]{1,0:T(8,128)S(1)} %get-tuple-element.9.x, f32[32,128]{1,0:T(8,128)S(1)} %get-tuple-element.10.y, f32[8,128]{1,0:T(8,128)S(1)} %get-tuple-element.11.weight), custom_call_target="tpu_custom_call" | custom-call | tf_op jit(solution)/shard_map/pallas_call | solution.py:675

commit v5 on v4

--- a/solution.py
+++ b/solution.py
@@ -41,6 +41,13 @@
         result = result + lax.rem(mine + theirs, 2) * bit
         bit *= 2
     return result
+
+
+def farthest(me, j, count):
+    upper = lax.div(me, (count + 1) // 2)
+    from_top = count - 1 - j - lax.div(me + j, count - 1)
+    from_bottom = j + lax.div(j + count - me, count)
+    return from_top + upper * (from_bottom - from_top)
 
 
 def repeat(first, count, call):
@@ -227,7 +234,7 @@
                 1,
                 count,
                 lambda k: send(
-                    axis, partner(me, count - k, count), mine, mine, leave.at[0], recvs.at[at]
+                    axis, farthest(me, k - 1, count), mine, mine, leave.at[0], recvs.at[at]
                 ),
             )
 
@@ -252,7 +259,7 @@
 
         def far():
             def one(k):
-                there = partner(outer, pairs - k, pairs) * 2 + inner
+                there = farthest(outer, k - 1, pairs) * 2 + inner
                 send("blk", there, ref.at[blk], ref.at[blk], all_send.at[0], recvs.at[outer])
 
             repeat(1, pairs, one)
@@ -433,7 +440,7 @@
         recv_sem = single()
 
         def one(k):
-            there = partner(outer, pairs - k, pairs)
+            there = farthest(outer, k - 1, pairs)
             send(
                 "blk",
                 there * 2 + inner,

time: 36.8 us -> 36.7 us (level)
  no operation moved by 1% of the time
where the time goes in v5:
time: 36.7 us; the launch traced here: 36.5 us
  Pallas kernels  35.8 us (98%)
  between operations  0.64 us (2%)
    pallas_call x1, Pallas kernels, shards(): pl.pallas_call(functools.partial(kernel, n_blk, n_grp), out_shape=(jax.Sh...  35.2 us

profile of v5, /device:TPU:0, one launch (start us, length us, event | category | flops | bytes accessed | tf_op | source)
XLA Modules:
  0.0 36.5 jit_solution(8816985360694591524)
XLA Ops:
  0.6 35.2 %shard_map.148 = (f32[64,128]{1,0:T(8,128)S(1)}, f32[32,128]{1,0:T(8,128)S(1)}, f32[8,128]{1,0:T(8,128)S(1)}) custom-call(f32[64,128]{1,0:T(8,128)} %bitcast.16, f32[32,128]{1,0:T(8,128)} %bitcast.21, f32[64,128]{1,0:T(8,128)} %bitcast.17, f32[64,128]{1,0:T(8,128)} %bitcast.18, f32[64,128]{1,0:T(8,128)} %bitcast.19, s32[64,128]{1,0:T(8,128)} %bitcast.20, ...), custom_call_target="tpu_custom_call" | custom-call | tf_op jit(solution)/shard_map/pallas_call | solution.py:614
  35.8 0.6 %shard_map.149 = (f32[64,128]{1,0:T(8,128)}, f32[32,128]{1,0:T(8,128)}, f32[1,1]{1,0:T(1,128)}) custom-call(f32[64,128]{1,0:T(8,128)S(1)} %get-tuple-element.9.x, f32[32,128]{1,0:T(8,128)S(1)} %get-tuple-element.10.y, f32[8,128]{1,0:T(8,128)S(1)} %get-tuple-element.11.weight), custom_call_target="tpu_custom_call" | custom-call | tf_op jit(solution)/shard_map/pallas_call | solution.py:682
